TPU v7x, 32 devices: a 4x4x1 block of a 4x4x8 slice. The times are simulated.
32 devices in a mesh: dp: 1 (over z), tp: 4 (over y), cp: 8 (over x, core).
Axes of the slice: x: 4, y: 4, z: 1, core: 2. Of those that a mesh axis runs over, the one named last changes fastest.
The devices are a block of a 4x4x8 slice.
Arguments:
- x: bfloat16 [8192, 5120], P(('dp', 'cp'))
- attn_gain: bfloat16 [5120], replicated
- w_q: bfloat16 [5120, 4096], P(None, 'tp')
- w_k: bfloat16 [5120, 1024], P(None, 'tp')
- w_v: bfloat16 [5120, 1024], P(None, 'tp')
- w_o: bfloat16 [4096, 5120], P('tp')
- mlp_gain: bfloat16 [5120], replicated
- w_gate: bfloat16 [5120, 14336], P(None, 'tp')
- w_up: bfloat16 [5120, 14336], P(None, 'tp')
- w_down: bfloat16 [14336, 5120], P('tp')
Outputs:
- output 1: bfloat16 [8192, 5120], P(('dp', 'cp'))
- output 2: bfloat16 [8192, 8, 128], P(('dp', 'cp'), 'tp')
- output 3: bfloat16 [8192, 8, 128], P(('dp', 'cp'), 'tp')
All inputs are finite; a program needn't handle non-finite values.
Results may differ from a plain program's by a relative error of at most 0.0135963.
Values are sent between devices in bfloat16 or wider.
A program may use at most 768 MiB of HBM per device.

v0:
```python
import math
import jax
import jax.numpy as jnp
from jax import lax
from jax.sharding import PartitionSpec as P

HEAD_DIM = 128
ROPE_THETA = 1000000.0
NORM_EPS = 1e-5
MASK_VALUE = -1e30
TILE_CAP = 512


def rms_norm(rows, gain):
    wide = rows.astype(jnp.float32)
    inv_rms = lax.rsqrt(jnp.mean(wide * wide, axis=-1, keepdims=True) + NORM_EPS)
    return (wide * inv_rms * gain.astype(jnp.float32)).astype(jnp.bfloat16)


def rope_tables(positions):
    inv_freq = jnp.asarray(ROPE_THETA, jnp.float32) ** (-jnp.arange(0, HEAD_DIM, 2, dtype=jnp.float32) / HEAD_DIM)
    angles = positions.astype(jnp.float32)[:, None] * inv_freq[None, :]
    return jnp.cos(angles), jnp.sin(angles)


def apply_rope(heads, cos_b, sin_b):
    half = heads.shape[-1] // 2
    wide = heads.astype(jnp.float32)
    first = wide[..., :half]
    second = wide[..., half:]
    return jnp.concatenate([first * cos_b - second * sin_b, second * cos_b + first * sin_b], axis=-1).astype(jnp.bfloat16)


def attend_tiles(state, queries, key_rows, value_rows, key_start, q_pos, n_tiles, tile):
    def tile_step(tile_idx, carry):
        run_max, run_sum, weighted = carry
        k_tile = lax.dynamic_slice_in_dim(key_rows, tile_idx * tile, tile, axis=0)
        v_tile = lax.dynamic_slice_in_dim(value_rows, tile_idx * tile, tile, axis=0)
        k_pos = key_start + tile_idx * tile + jnp.arange(tile)
        scores = jnp.einsum('qkgd,skd->kgqs', queries, k_tile, preferred_element_type=jnp.float32) * (HEAD_DIM ** -0.5)
        scores = jnp.where(k_pos[None, :] <= q_pos[:, None], scores, MASK_VALUE)
        new_max = jnp.maximum(run_max, jnp.max(scores, axis=-1))
        rescale = jnp.exp(run_max - new_max)
        exp_scores = jnp.exp(scores - new_max[..., None])
        new_sum = run_sum * rescale + jnp.sum(exp_scores, axis=-1)
        new_weighted = weighted * rescale[..., None] + jnp.einsum('kgqs,skd->kgqd', exp_scores.astype(jnp.bfloat16), v_tile, preferred_element_type=jnp.float32)
        return new_max, new_sum, new_weighted
    return lax.fori_loop(0, n_tiles, tile_step, state)


def solution(mesh):
    cp_size = mesh.shape['cp']
    shift_pairs = [(source, (source + 1) % cp_size) for source in range(cp_size)]
    row_spec = P(('dp', 'cp'), None)
    cache_spec = P(('dp', 'cp'), 'tp', None)
    col_spec = P(None, 'tp')
    split_rows = P('tp', None)
    vec_spec = P(None)

    def local_layer(x, attn_gain, w_q, w_k, w_v, w_o, mlp_gain, w_gate, w_up, w_down):
        tok_dev = x.shape[0]
        kv_local = w_k.shape[1] // HEAD_DIM
        groups = w_q.shape[1] // w_k.shape[1]
        cp_index = lax.axis_index('cp')
        q_pos = cp_index * tok_dev + jnp.arange(tok_dev)
        cos_tab, sin_tab = rope_tables(q_pos)
        normed = rms_norm(x, attn_gain)
        queries = jnp.dot(normed, w_q, preferred_element_type=jnp.float32).astype(jnp.bfloat16).reshape(tok_dev, kv_local, groups, HEAD_DIM)
        keys = jnp.dot(normed, w_k, preferred_element_type=jnp.float32).astype(jnp.bfloat16).reshape(tok_dev, kv_local, HEAD_DIM)
        values = jnp.dot(normed, w_v, preferred_element_type=jnp.float32).astype(jnp.bfloat16).reshape(tok_dev, kv_local, HEAD_DIM)
        queries = apply_rope(queries, cos_tab[:, None, None, :], sin_tab[:, None, None, :])
        keys = apply_rope(keys, cos_tab[:, None, :], sin_tab[:, None, :])
        tile = math.gcd(tok_dev, TILE_CAP)
        n_tiles = tok_dev // tile
        stat_shape = (kv_local, groups, tok_dev)
        state = (jnp.full(stat_shape, MASK_VALUE, jnp.float32), jnp.zeros(stat_shape, jnp.float32), jnp.zeros(stat_shape + (HEAD_DIM,), jnp.float32))
        state = attend_tiles(state, queries, keys, values, cp_index * tok_dev, q_pos, n_tiles, tile)

        def shift_step(step, carry):
            held, state_in = carry
            held = lax.ppermute(held, 'cp', shift_pairs)
            source = cp_index - step

            def use_block(current):
                return attend_tiles(current, queries, held[0], held[1], source * tok_dev, q_pos, n_tiles, tile)

            def keep_state(current):
                return current

            state_out = lax.cond(step <= cp_index, use_block, keep_state, state_in)
            return held, state_out

        state = lax.fori_loop(1, cp_size, shift_step, ((keys, values), state))[1]
        attn_heads = (state[2] / state[1][..., None]).astype(jnp.bfloat16)
        attn_rows = jnp.transpose(attn_heads, (2, 0, 1, 3)).reshape(tok_dev, kv_local * groups * HEAD_DIM)
        attn_part = jnp.dot(attn_rows, w_o, preferred_element_type=jnp.float32).astype(jnp.bfloat16)
        attn_total = lax.psum(attn_part, 'tp')
        hidden = (x.astype(jnp.float32) + attn_total.astype(jnp.float32)).astype(jnp.bfloat16)
        normed_mlp = rms_norm(hidden, mlp_gain)
        gate_proj = jnp.dot(normed_mlp, w_gate, preferred_element_type=jnp.float32)
        up_proj = jnp.dot(normed_mlp, w_up, preferred_element_type=jnp.float32)
        activated = (jax.nn.silu(gate_proj) * up_proj).astype(jnp.bfloat16)
        down_part = jnp.dot(activated, w_down, preferred_element_type=jnp.float32).astype(jnp.bfloat16)
        down_total = lax.psum(down_part, 'tp')
        x_out = (hidden.astype(jnp.float32) + down_total.astype(jnp.float32)).astype(jnp.bfloat16)
        return x_out, keys, values

    return jax.shard_map(local_layer, mesh=mesh,
                         in_specs=(row_spec, vec_spec, col_spec, col_spec, col_spec, split_rows, vec_spec, col_spec, col_spec, split_rows),
                         out_specs=(row_spec, cache_spec, cache_spec), check_vma=False)
```

profile of v0, /device:TPU:103, one launch (start us, length us, event | category | flops | bytes accessed | tf_op | source)
XLA Modules:
  0.0 1195.2 jit_solution(10503500759781993609)
XLA Ops:
  38.5 17.0 %convolution_convert_fusion.2 = bf16[1024,1024]{0,1:T(8,128)(2,1)S(1)} fusion(bf16[5120,1024]{1,0:T(8,128)(2,1)} %param.20, bf16[1024,5120]{1,0:T(8,128)(2,1)} %param.18, f32[5120]{0:T(1024)S(1)} %convert_element_type.96, f32[1024]{0:T(1024)S(1)} %add_rsqrt_fusion.1), kind=kOutput, calls=%fused_computation.71 | convolution fusion | flops 10759438336 | bytes 23093248 | tf_op jit(solution)/shard_map/dot_general | solution.py:68
  72.0 55.1 %while.60 = (s32[]{:T(128)}, f32[2,4,1024]{2,1,0:T(4,128)S(1)}, f32[2,4,1024]{2,1,0:T(4,128)S(1)}, f32[2,4,1024,128]{3,2,1,0:T(8,128)}, s32[]{:T(128)}, /*index=...) while((s32[]{:T(128)}, f32[2,4,1024]{2,1,0:T(4,128)S(1)}, ...), condition=%wide.region_4.5_spmd.clone.clone.clone, body=%wide.region_1.4_spmd.clone.clone.clone.sunk | while | flops 2197333504 | bytes 63975632 | solution.py:48
  79.7 9.2 fusion.84
  89.0 10.0 fusion.86
  106.7 9.2 fusion.84
  116.0 11.1 fusion.86
  127.1 493.9 %while.59 = (s32[]{:T(128)}, bf16[1024,2,128]{2,0,1:T(8,128)(2,1)S(1)}, bf16[1024,2,128]{2,0,1:T(8,128)(2,1)}, f32[2,4,1024]{2,1,0:T(4,128)S(1)}, f32[2,4,1024]{...) while((s32[]{:T(128)}, ...), condition=%wide.region_12.13_spmd.clone, body=%wide.region_5.12_spmd.clone.sunk | while | flops 2196260352 | bytes 70275736 | solution.py:93
  139.9 56.0 %conditional.3 = ((f32[2,4,1024]{2,1,0:T(4,128)S(1)}, f32[2,4,1024]{2,1,0:T(4,128)S(1)}, f32[2,4,1024,128]{3,2,1,0:T(8,128)})) conditional(s32[]{:T(128)} %convert_element_type.183, (f32[2,4,1024]{2,1,0:T(4,128)S(1)}, f32[2,4,1024]{2,1,0:T(4,128)S(1)}, f32[2,4,1024,128]{3,2,1,0:T(8,128)}) %tuple.121, (s32[]{:T(128)}, s32[]{:T(128)}, s32[]{:T(128)}, ...), branch_computations={%region_6.6_spmd, %region_7.11_spmd} | conditional | flops 2196260352 | bytes 63979888 | solution.py:90
  139.9 56.0 %while.58 = (s32[]{:T(128)}, f32[2,4,1024]{2,1,0:T(4,128)S(1)}, f32[2,4,1024]{2,1,0:T(4,128)S(1)}, f32[2,4,1024,128]{3,2,1,0:T(8,128)}, s32[]{:T(128)}, /*index=...) while((s32[]{:T(128)}, f32[2,4,1024]{2,1,0:T(4,128)S(1)}, ...), condition=%wide.region_11.10_spmd, body=%wide.region_8.9_spmd.sunk | while | flops 2196259328 | bytes 63971524 | solution.py:48
  147.6 9.2 fusion.91
  156.8 11.0 multiply_add_fusion.5
  175.5 9.2 fusion.91
  184.8 11.0 multiply_add_fusion.5
  209.6 56.0 %conditional.3 = ((f32[2,4,1024]{2,1,0:T(4,128)S(1)}, f32[2,4,1024]{2,1,0:T(4,128)S(1)}, f32[2,4,1024,128]{3,2,1,0:T(8,128)})) conditional(s32[]{:T(128)} %convert_element_type.183, (f32[2,4,1024]{2,1,0:T(4,128)S(1)}, f32[2,4,1024]{2,1,0:T(4,128)S(1)}, f32[2,4,1024,128]{3,2,1,0:T(8,128)}) %tuple.121, (s32[]{:T(128)}, s32[]{:T(128)}, s32[]{:T(128)}, ...), branch_computations={%region_6.6_spmd, %region_7.11_spmd} | conditional | flops 2196260352 | bytes 63979888 | solution.py:90
  209.6 56.0 %while.58 = (s32[]{:T(128)}, f32[2,4,1024]{2,1,0:T(4,128)S(1)}, f32[2,4,1024]{2,1,0:T(4,128)S(1)}, f32[2,4,1024,128]{3,2,1,0:T(8,128)}, s32[]{:T(128)}, /*index=...) while((s32[]{:T(128)}, f32[2,4,1024]{2,1,0:T(4,128)S(1)}, ...), condition=%wide.region_11.10_spmd, body=%wide.region_8.9_spmd.sunk | while | flops 2196259328 | bytes 63971524 | solution.py:48
  226.5 11.0 multiply_add_fusion.5
  254.5 11.0 multiply_add_fusion.5
  279.3 56.0 %conditional.3 = ((f32[2,4,1024]{2,1,0:T(4,128)S(1)}, f32[2,4,1024]{2,1,0:T(4,128)S(1)}, f32[2,4,1024,128]{3,2,1,0:T(8,128)})) conditional(s32[]{:T(128)} %convert_element_type.183, (f32[2,4,1024]{2,1,0:T(4,128)S(1)}, f32[2,4,1024]{2,1,0:T(4,128)S(1)}, f32[2,4,1024,128]{3,2,1,0:T(8,128)}) %tuple.121, (s32[]{:T(128)}, s32[]{:T(128)}, s32[]{:T(128)}, ...), branch_computations={%region_6.6_spmd, %region_7.11_spmd} | conditional | flops 2196260352 | bytes 63979888 | solution.py:90
  279.3 56.0 %while.58 = (s32[]{:T(128)}, f32[2,4,1024]{2,1,0:T(4,128)S(1)}, f32[2,4,1024]{2,1,0:T(4,128)S(1)}, f32[2,4,1024,128]{3,2,1,0:T(8,128)}, s32[]{:T(128)}, /*index=...) while((s32[]{:T(128)}, f32[2,4,1024]{2,1,0:T(4,128)S(1)}, ...), condition=%wide.region_11.10_spmd, body=%wide.region_8.9_spmd.sunk | while | flops 2196259328 | bytes 63971524 | solution.py:48
  296.2 11.0 multiply_add_fusion.5
  324.2 11.0 multiply_add_fusion.5
  349.0 56.0 %conditional.3 = ((f32[2,4,1024]{2,1,0:T(4,128)S(1)}, f32[2,4,1024]{2,1,0:T(4,128)S(1)}, f32[2,4,1024,128]{3,2,1,0:T(8,128)})) conditional(s32[]{:T(128)} %convert_element_type.183, (f32[2,4,1024]{2,1,0:T(4,128)S(1)}, f32[2,4,1024]{2,1,0:T(4,128)S(1)}, f32[2,4,1024,128]{3,2,1,0:T(8,128)}) %tuple.121, (s32[]{:T(128)}, s32[]{:T(128)}, s32[]{:T(128)}, ...), branch_computations={%region_6.6_spmd, %region_7.11_spmd} | conditional | flops 2196260352 | bytes 63979888 | solution.py:90
  349.0 56.0 %while.58 = (s32[]{:T(128)}, f32[2,4,1024]{2,1,0:T(4,128)S(1)}, f32[2,4,1024]{2,1,0:T(4,128)S(1)}, f32[2,4,1024,128]{3,2,1,0:T(8,128)}, s32[]{:T(128)}, /*index=...) while((s32[]{:T(128)}, f32[2,4,1024]{2,1,0:T(4,128)S(1)}, ...), condition=%wide.region_11.10_spmd, body=%wide.region_8.9_spmd.sunk | while | flops 2196259328 | bytes 63971524 | solution.py:48
  365.9 11.0 multiply_add_fusion.5
  393.9 11.0 multiply_add_fusion.5
  407.0 10.9 collective-permute-done.1
  418.8 56.0 %conditional.3 = ((f32[2,4,1024]{2,1,0:T(4,128)S(1)}, f32[2,4,1024]{2,1,0:T(4,128)S(1)}, f32[2,4,1024,128]{3,2,1,0:T(8,128)})) conditional(s32[]{:T(128)} %convert_element_type.183, (f32[2,4,1024]{2,1,0:T(4,128)S(1)}, f32[2,4,1024]{2,1,0:T(4,128)S(1)}, f32[2,4,1024,128]{3,2,1,0:T(8,128)}) %tuple.121, (s32[]{:T(128)}, s32[]{:T(128)}, s32[]{:T(128)}, ...), branch_computations={%region_6.6_spmd, %region_7.11_spmd} | conditional | flops 2196260352 | bytes 63979888 | solution.py:90
  418.8 56.0 %while.58 = (s32[]{:T(128)}, f32[2,4,1024]{2,1,0:T(4,128)S(1)}, f32[2,4,1024]{2,1,0:T(4,128)S(1)}, f32[2,4,1024,128]{3,2,1,0:T(8,128)}, s32[]{:T(128)}, /*index=...) while((s32[]{:T(128)}, f32[2,4,1024]{2,1,0:T(4,128)S(1)}, ...), condition=%wide.region_11.10_spmd, body=%wide.region_8.9_spmd.sunk | while | flops 2196259328 | bytes 63971524 | solution.py:48
  435.7 11.0 multiply_add_fusion.5
  463.7 11.0 multiply_add_fusion.5
  476.8 13.3 %collective-permute-done.1 = bf16[1024,2,128]{2,0,1:T(8,128)(2,1)} collective-permute-done((bf16[1024,2,128]{2,0,1:T(8,128)(2,1)}, bf16[1024,2,128]{2,0,1:T(8,128)(2,1)}, u32[]{:S(2)}, u32[]{:S(2)}) %collective-permute-start.1) | collective-permute-done | bytes 524320 | tf_op jit(solution)/shard_map/while/body/eval_jaxpr/ppermute | solution.py:81
  490.9 56.0 %conditional.3 = ((f32[2,4,1024]{2,1,0:T(4,128)S(1)}, f32[2,4,1024]{2,1,0:T(4,128)S(1)}, f32[2,4,1024,128]{3,2,1,0:T(8,128)})) conditional(s32[]{:T(128)} %convert_element_type.183, (f32[2,4,1024]{2,1,0:T(4,128)S(1)}, f32[2,4,1024]{2,1,0:T(4,128)S(1)}, f32[2,4,1024,128]{3,2,1,0:T(8,128)}) %tuple.121, (s32[]{:T(128)}, s32[]{:T(128)}, s32[]{:T(128)}, ...), branch_computations={%region_6.6_spmd, %region_7.11_spmd} | conditional | flops 2196260352 | bytes 63979888 | solution.py:90
  490.9 56.0 %while.58 = (s32[]{:T(128)}, f32[2,4,1024]{2,1,0:T(4,128)S(1)}, f32[2,4,1024]{2,1,0:T(4,128)S(1)}, f32[2,4,1024,128]{3,2,1,0:T(8,128)}, s32[]{:T(128)}, /*index=...) while((s32[]{:T(128)}, f32[2,4,1024]{2,1,0:T(4,128)S(1)}, ...), condition=%wide.region_11.10_spmd, body=%wide.region_8.9_spmd.sunk | while | flops 2196259328 | bytes 63971524 | solution.py:48
  507.9 11.0 multiply_add_fusion.5
  535.9 11.0 multiply_add_fusion.5
  549.0 13.3 %collective-permute-done.1 = bf16[1024,2,128]{2,0,1:T(8,128)(2,1)} collective-permute-done((bf16[1024,2,128]{2,0,1:T(8,128)(2,1)}, bf16[1024,2,128]{2,0,1:T(8,128)(2,1)}, u32[]{:S(2)}, u32[]{:S(2)}) %collective-permute-start.1) | collective-permute-done | bytes 524320 | tf_op jit(solution)/shard_map/while/body/eval_jaxpr/ppermute | solution.py:81
  563.1 56.0 %conditional.3 = ((f32[2,4,1024]{2,1,0:T(4,128)S(1)}, f32[2,4,1024]{2,1,0:T(4,128)S(1)}, f32[2,4,1024,128]{3,2,1,0:T(8,128)})) conditional(s32[]{:T(128)} %convert_element_type.183, (f32[2,4,1024]{2,1,0:T(4,128)S(1)}, f32[2,4,1024]{2,1,0:T(4,128)S(1)}, f32[2,4,1024,128]{3,2,1,0:T(8,128)}) %tuple.121, (s32[]{:T(128)}, s32[]{:T(128)}, s32[]{:T(128)}, ...), branch_computations={%region_6.6_spmd, %region_7.11_spmd} | conditional | flops 2196260352 | bytes 63979888 | solution.py:90
  563.1 56.0 %while.58 = (s32[]{:T(128)}, f32[2,4,1024]{2,1,0:T(4,128)S(1)}, f32[2,4,1024]{2,1,0:T(4,128)S(1)}, f32[2,4,1024,128]{3,2,1,0:T(8,128)}, s32[]{:T(128)}, /*index=...) while((s32[]{:T(128)}, f32[2,4,1024]{2,1,0:T(4,128)S(1)}, ...), condition=%wide.region_11.10_spmd, body=%wide.region_8.9_spmd.sunk | while | flops 2196259328 | bytes 63971524 | solution.py:48
  580.1 11.0 multiply_add_fusion.5
  608.0 11.0 multiply_add_fusion.5
  629.3 17.3 %convolution_convert_fusion = bf16[1024,5120]{1,0:T(8,128)(2,1)} fusion(bf16[1024,1024]{0,1:T(8,128)(2,1)S(1)} %bitcast.114, bf16[1024,5120]{1,0:T(8,128)(2,1)} %param.23), kind=kOutput, calls=%fused_computation.64 | convolution fusion | flops 10742661120 | bytes 23068672 | tf_op jit(solution)/shard_map/dot_general | solution.py:96
  647.3 190.1 %all-reduce.3.cloned.1.call-done = bf16[1024,5120]{1,0:T(8,128)(2,1)} async-done(((bf16[1024,5120]{1,0:T(8,128)(2,1)}), bf16[1024,5120]{1,0:T(8,128)(2,1)}) %all-reduce.3.cloned.1.call-update) | async-done | bytes 10485776 | tf_op jit(solution)/shard_map/psum | solution.py:97
  837.4 9.6 fusion.44
  847.0 47.0 %fusion.49 = f32[1024,3584]{1,0:T(8,128)} fusion(bf16[5120,3584]{1,0:T(8,128)(2,1)} %param.25, bf16[1024,5120]{1,0:T(8,128)(2,1)S(1)} %get-tuple-element.717, f32[5120]{0:T(1024)S(1)} %convert_element_type.111, f32[1024]{0:T(1024)S(1)} %add_rsqrt_fusion), kind=kOutput, calls=%fused_computation.69 | convolution fusion | flops 37601935360 | bytes 61890560 | tf_op jit(solution)/shard_map/dot_general | solution.py:100
  894.1 45.2 %multiply_convert_fusion = bf16[1024,3584]{1,0:T(8,128)(2,1)} fusion(f32[1024,3584]{1,0:T(8,128)} %fusion.49, bf16[5120,3584]{1,0:T(8,128)(2,1)} %param.26, bf16[1024,5120]{1,0:T(8,128)(2,1)S(1)} %get-tuple-element.717, f32[5120]{0:T(1024)S(1)} %convert_element_type.111, f32[1024]{0:T(1024)S(1)} %add_rsqrt_fusion), kind=kOutput, calls=%fused_computation.63 | convolution fusion | flops 37623955456 | bytes 69230592 | tf_op jit(solution)/shard_map/dot_general | solution.py:101
  939.3 45.6 %convolution_convert_fusion.1 = bf16[1024,5120]{1,0:T(8,128)(2,1)} fusion(bf16[1024,3584]{1,0:T(8,128)(2,1)} %multiply_convert_fusion, bf16[3584,5120]{1,0:T(8,128)(2,1)} %param.27), kind=kOutput, calls=%fused_computation.65 | convolution fusion | flops 37586206720 | bytes 54525952 | tf_op jit(solution)/shard_map/dot_general | solution.py:103
  987.1 186.7 %all-reduce.5.cloned.1.call-done = bf16[1024,5120]{1,0:T(8,128)(2,1)} async-done(((bf16[1024,5120]{1,0:T(8,128)(2,1)}), bf16[1024,5120]{1,0:T(8,128)(2,1)}) %all-reduce.5.cloned.1.call-update) | async-done | bytes 10485776 | tf_op jit(solution)/shard_map/psum | solution.py:104
  1173.8 14.1 %fusion.47 = bf16[1024,5120]{1,0:T(8,128)(2,1)} fusion(bf16[1024,5120]{1,0:T(8,128)(2,1)} %copy-done.2, bf16[1024,5120]{1,0:T(8,128)(2,1)} %all-reduce.5.cloned.1.call-done), kind=kLoop, calls=%fused_computation.62 | loop fusion | flops 20971520 | bytes 31457280 | tf_op jit(solution)/shard_map/convert_element_type | solution.py:105
  (215 shorter events, 356.6 us)
Async XLA Ops:
  7.2 6.4 copy-start
  7.2 6.4 copy-start.8
  7.2 830.2 %all-reduce.3.cloned.1.call-start = ((), (), s32[]{:S(2)}) async-start(), calls=%async_computation | async-start | bytes 20971520 | tf_op jit(solution)/shard_map/psum | solution.py:97
  20.8 9.0 copy-start.6
  33.9 3.8 copy-start.3
  37.7 0.8 copy-start.5
  58.1 8.0 copy-start.4
  127.2 7.0 collective-permute-start.1
  128.2 11.7 collective-permute-start
  197.8 6.2 collective-permute-start.1
  197.9 11.7 collective-permute-start
  267.5 6.2 collective-permute-start.1
  267.6 11.7 collective-permute-start
  337.2 8.6 collective-permute-start.1
  337.3 11.7 collective-permute-start
  406.9 11.1 collective-permute-start.1
  407.0 11.8 collective-permute-start
  476.7 13.5 %collective-permute-start.1 = (bf16[1024,2,128]{2,0,1:T(8,128)(2,1)}, bf16[1024,2,128]{2,0,1:T(8,128)(2,1)}, u32[]{:S(2)}, u32[]{:S(2)}) collective-permute-start(bf16[1024,2,128]{2,0,1:T(8,128)(2,1)} %get-tuple-element.1010), channel_id=1, source_target_pairs={{0,1},{1,2},{2,3},{3,4},{4,5},{5,6},{6,7},{7,0},{8,9},{9,10},{10,1... | collective-permute-start | bytes 1572872 | tf_op jit(solution)/shard_map/while/body/eval_jaxpr/ppermute | solution.py:81
  476.7 14.2 %collective-permute-start = (bf16[1024,2,128]{2,0,1:T(8,128)(2,1)S(1)}, bf16[1024,2,128]{2,0,1:T(8,128)(2,1)S(1)}, u32[]{:S(2)}, u32[]{:S(2)}) collective-permute-start(bf16[1024,2,128]{2,0,1:T(8,128)(2,1)S(1)} %get-tuple-element.1009), channel_id=1, source_target_pairs={{0,1},{1,2},{2,3},{3,4},{4,5},{5,6},{6,7},{7,0},{8,9},{9,10},{10,1... | collective-permute-start | bytes 1572872 | tf_op jit(solution)/shard_map/while/body/eval_jaxpr/ppermute | solution.py:81
  548.8 13.5 %collective-permute-start.1 = (bf16[1024,2,128]{2,0,1:T(8,128)(2,1)}, bf16[1024,2,128]{2,0,1:T(8,128)(2,1)}, u32[]{:S(2)}, u32[]{:S(2)}) collective-permute-start(bf16[1024,2,128]{2,0,1:T(8,128)(2,1)} %get-tuple-element.1010), channel_id=1, source_target_pairs={{0,1},{1,2},{2,3},{3,4},{4,5},{5,6},{6,7},{7,0},{8,9},{9,10},{10,1... | collective-permute-start | bytes 1572872 | tf_op jit(solution)/shard_map/while/body/eval_jaxpr/ppermute | solution.py:81
  548.9 14.2 %collective-permute-start = (bf16[1024,2,128]{2,0,1:T(8,128)(2,1)S(1)}, bf16[1024,2,128]{2,0,1:T(8,128)(2,1)S(1)}, u32[]{:S(2)}, u32[]{:S(2)}) collective-permute-start(bf16[1024,2,128]{2,0,1:T(8,128)(2,1)S(1)} %get-tuple-element.1009), channel_id=1, source_target_pairs={{0,1},{1,2},{2,3},{3,4},{4,5},{5,6},{6,7},{7,0},{8,9},{9,10},{10,1... | collective-permute-start | bytes 1572872 | tf_op jit(solution)/shard_map/while/body/eval_jaxpr/ppermute | solution.py:81
  646.6 0.7 copy-start.9
  646.6 527.1 %all-reduce.5.cloned.1.call-start = ((), (), s32[]{:S(2)}) async-start(), calls=%async_computation.1 | async-start | bytes 20971520 | tf_op jit(solution)/shard_map/psum | solution.py:104
  847.0 47.1 %copy-start.2 = (bf16[1024,5120]{1,0:T(8,128)(2,1)}, bf16[1024,5120]{1,0:T(8,128)(2,1)S(1)}, u32[]{:S(2)}) copy-start(bf16[1024,5120]{1,0:T(8,128)(2,1)S(1)} %get-tuple-element.717) | copy-start | bytes 31457284
  984.9 1.0 copy-start.7
  986.0 202.0 %copy-start.1 = (bf16[5120,256]{1,0:T(8,128)(2,1)S(1)}, bf16[5120,256]{1,0:T(8,128)(2,1)}, u32[]{:S(2)}) copy-start(bf16[5120,256]{1,0:T(8,128)(2,1)} %param.22) | copy-start | bytes 7864324
Sparse Core Ops, SparseCore 0:
  646.8 190.5 all-reduce.2
  985.1 188.6 all-reduce.4
where the time goes:
time: 1200 us
  matrix products  480 us (40%)
  waiting for transfers between devices  462 us (38%)
  other arithmetic  199 us (17%)
  local copies, waits for them, and re-layouts  36.2 us (3%)
  between operations  14.8 us (1%)
    psum x1, waiting for transfers between devices, local_layer(): attn_total = lax.psum(attn_part, 'tp')  190 us
    psum x1, waiting for transfers between devices, local_layer(): down_total = lax.psum(down_part, 'tp')  187 us
    dot_general x16, matrix products, tile_step(): jnp.einsum('kgqs,skd->kgqd', exp_scores.astype(jnp.bfloat16), v_tile, pre...  176 us
    reduce_sum x16, other arithmetic, tile_step(): new_sum = run_sum * rescale + jnp.sum(exp_scores, axis=-1)  148 us
    dot_general x16, matrix products, tile_step(): jnp.einsum('qkgd,skd->kgqs', queries, k_tile, preferred_element_type=jnp....  116 us
    ppermute x14, waiting for transfers between devices, shift_step(): held = lax.ppermute(held, 'cp', shift_pairs)  85.5 us
    dot_general x1, matrix products, local_layer(): gate_proj = jnp.dot(normed_mlp, w_gate, preferred_element_type=jnp.float32)  47 us
    dot_general x1, matrix products, local_layer(): jnp.dot(activated, w_down, preferred_element_type=jnp.float32)  45.6 us
  transfers between devices with their start and end apart: 16, of which 16 were waited for; matrix products, arithmetic and copies ran while one was open for 0% of the time, Pallas kernels for 0%

commit v1 on v0

v1 whole, which is shorter than its diff:
```python
import functools
import math
import jax
import jax.numpy as jnp
from jax import lax
from jax.experimental import pallas as pl
from jax.experimental.pallas import tpu as pltpu
from jax.sharding import PartitionSpec as P

HEAD_DIM = 128
ROPE_THETA = 1000000.0
NORM_EPS = 1e-5
MASK_VALUE = -1e30
VMEM_LIMIT = 66000000
HALVES = 2
GROUPS_OUT = 4
FF_TILE = 256
OUT_TILE = 256
PROJ_TILE = 256
Q_CHUNKS = 4
KEY_TILE = 512
OUT_COLS = 1024
NORM_ROWS = 64


def attn_kernel(n_tp, n_cp, x_hbm, gain_ref, mlp_gain_ref, cos_ref, sin_ref, wq_hbm, wk_hbm, wv_hbm, wo_hbm,
                k_out, v_out, h_out, n_out,
                nbuf, wt, kbuf, vbuf, qt, part, relay, fin, hrow, nrow, orow, acc, m_st, l_st, knat, vnat,
                xsem, wsem, wosem, hsem, osem, kvo_sem, kx_send, kx_recv, sb_send, sb_recv, rs_send, rs_recv):
    tok, D = nbuf.shape
    kv_n, groups = kbuf.shape[2], qt.shape[3] // (tok // Q_CHUNKS)
    QC = tok // Q_CHUNKS
    QL = qt.shape[3]
    R = QC // n_tp
    H = R // 2
    lo, hi = pl.ds(0, H), pl.ds(H, H)
    me = lax.axis_index('tp')
    right = lax.rem(me + 1, n_tp)
    left = lax.rem(me + n_tp - 1, n_tp)
    far = lax.rem(me + 2, n_tp)
    cp = lax.axis_index('cp')
    core = lax.rem(cp, 2)
    chip = cp // 2
    sib = cp + 1 - 2 * core
    x_right = lax.rem(cp + 2, n_cp)
    x_left = lax.rem(cp + n_cp - 2, n_cp)
    cexp = (HEAD_DIM ** -0.5) * math.log2(math.e)
    f32, bf16 = jnp.float32, jnp.bfloat16

    def remote(src, dst, ssem, rsem, to):
        return pltpu.make_async_remote_copy(src_ref=src, dst_ref=dst, send_sem=ssem, recv_sem=rsem,
                                            device_id=to, device_id_type=pl.DeviceIdType.MESH)

    def kx(k):
        buf, src, dst, to = ((kbuf, 0, 1, x_right), (vbuf, 0, 1, x_right), (vbuf, 0, 2, x_left), (kbuf, 0, 2, x_left),
                             (kbuf, 1, 3, x_right), (vbuf, 2, 3, x_left))[k]
        return remote(buf.at[src, 0], buf.at[dst, 0], kx_send.at[k], kx_recv.at[k], {'cp': to})

    def sb(rel, b):
        buf = (kbuf, vbuf)[b]
        return remote(buf.at[rel, 0], buf.at[rel, 1], sb_send.at[rel, b], sb_recv.at[rel, b], {'cp': sib})

    def rs(i, k):
        p = lax.rem(i, 2)
        src, dst, to = ((part.at[p, far, lo], relay.at[i, 0], right),
                        (part.at[p, far, hi], relay.at[i, 1], left),
                        (part.at[p, right, hi], fin.at[i, 0, hi], right),
                        (part.at[p, left, lo], fin.at[i, 1, lo], left),
                        (part.at[p, right, lo], fin.at[i, 0, lo], right),
                        (part.at[p, left, hi], fin.at[i, 1, hi], left))[k]
        return remote(src, dst, rs_send.at[i, k], rs_recv.at[i, k], {'tp': to})

    def x_load(c):
        rows = pl.ds(c * QC, QC)
        return pltpu.make_async_copy(x_hbm.at[rows], nbuf.at[rows], xsem.at[c])

    def w_load(ref, t, slot):
        return pltpu.make_async_copy(ref.at[:, pl.ds(pl.multiple_of(t * PROJ_TILE, PROJ_TILE), PROJ_TILE)], wt.at[slot], wsem.at[slot])

    def h_load(i):
        return pltpu.make_async_copy(x_hbm.at[pl.ds(pl.multiple_of(i * QC + me * R, R), R)], hrow.at[i], hsem.at[i])

    def o_store(i):
        rows = pl.ds(i * R, R)
        return (pltpu.make_async_copy(hrow.at[i], h_out.at[rows], osem.at[0, i]),
                pltpu.make_async_copy(nrow.at[i], n_out.at[rows], osem.at[1, i]))

    wo_load = pltpu.make_async_copy(wo_hbm, nbuf, wosem)

    for c in range(Q_CHUNKS):
        x_load(c).start()
    w_load(wk_hbm, 0, 0).start()
    w_load(wv_hbm, 0, 1).start()
    for i in range(Q_CHUNKS):
        h_load(i).start()
    barrier = pltpu.get_barrier_semaphore()
    for to in ({'tp': left}, {'tp': right}, {'cp': x_left}, {'cp': x_right}, {'cp': sib}):
        pl.semaphore_signal(barrier, inc=1, device_id=to, device_id_type=pl.DeviceIdType.MESH)
    pl.semaphore_wait(barrier, 5)

    def normalize(wide, gain):
        inv = lax.rsqrt(jnp.mean(wide * wide, axis=-1, keepdims=True) + NORM_EPS)
        return (wide * inv * gain).astype(bf16)

    gain = gain_ref[...].astype(f32)
    for c in range(Q_CHUNKS):
        x_load(c).wait()

        def norm_step(b, carry):
            rows = pl.ds(pl.multiple_of(c * QC + b * NORM_ROWS, NORM_ROWS), NORM_ROWS)
            nbuf[rows, :] = normalize(nbuf[rows, :].astype(f32), gain)
            return carry
        lax.fori_loop(0, QC // NORM_ROWS, norm_step, 0)

    def rope(u):
        wide = u.astype(bf16).astype(f32)
        return (wide * cos_ref[...] + pltpu.roll(wide, HEAD_DIM // 2, 1) * sin_ref[...]).astype(bf16)

    def project(slot):
        return jnp.dot(nbuf[...], wt[slot], preferred_element_type=f32)

    w_load(wk_hbm, 0, 0).wait()
    res = project(0)
    for j in range(kv_n):
        head = rope(res[:, j * HEAD_DIM:(j + 1) * HEAD_DIM])
        kbuf[0, 0, j] = head
        knat[:, j * HEAD_DIM:(j + 1) * HEAD_DIM] = head
    w_load(wq_hbm, 0, 0).start()
    w_load(wv_hbm, 0, 1).wait()
    kx(0).start()
    kx(3).start()
    sb(0, 0).start()
    res = project(1).astype(bf16)
    vnat[...] = res
    for j in range(kv_n):
        vbuf[0, 0, j] = res[:, j * HEAD_DIM:(j + 1) * HEAD_DIM].T
    w_load(wq_hbm, 1, 1).start()
    pltpu.make_async_copy(knat, k_out, kvo_sem.at[0]).start()
    kx(1).start()
    kx(2).start()
    sb(0, 1).start()
    pltpu.make_async_copy(vnat, v_out, kvo_sem.at[1]).start()

    n_q = wq_hbm.shape[1] // PROJ_TILE
    heads_tile = PROJ_TILE // HEAD_DIM
    tiles_kv = n_q // kv_n

    def q_step(t, carry):
        slot = lax.rem(t, 2)
        w_load(wq_hbm, t, slot).wait()
        res = project(slot)
        kv, base = t // tiles_kv, lax.rem(t, tiles_kv) * heads_tile
        for j in range(heads_tile):
            head = rope(res[:, j * HEAD_DIM:(j + 1) * HEAD_DIM])
            lanes = pl.ds(pl.multiple_of((base + j) * QC, QC), QC)
            for i in range(Q_CHUNKS):
                qt[i, kv, :, lanes] = head[i * QC:(i + 1) * QC].T

        @pl.when(t + 2 < n_q)
        def _():
            w_load(wq_hbm, t + 2, slot).start()

        @pl.when(t == n_q - 1)
        def _():
            kx(0).wait_recv()
            kx(4).start()
            sb(1, 0).start()
            kx(2).wait_recv()
            kx(5).start()
            sb(2, 1).start()
        return carry
    lax.fori_loop(0, n_q, q_step, 0)
    wo_load.start()

    def attend(i, kv, k_tile, v_tile, masked):
        s = jnp.dot(k_tile, qt[i, kv], preferred_element_type=f32)
        if masked:
            key = lax.broadcasted_iota(jnp.int32, s.shape, 0)
            row = lax.broadcasted_iota(jnp.int32, s.shape, 1) & (QC - 1)
            s = jnp.where(key <= row, s, MASK_VALUE)
        m_old = m_st[kv]
        m_new = jnp.maximum(m_old, jnp.max(s, axis=0, keepdims=True))
        alpha = jnp.exp2((m_old - m_new) * cexp)
        p = jnp.exp2((s - m_new) * cexp)
        m_st[kv] = m_new
        l_st[kv] = l_st[kv] * alpha + jnp.sum(p, axis=0, keepdims=True)
        acc[kv] = acc[kv] * alpha + jnp.dot(v_tile, p.astype(bf16), preferred_element_type=f32)

    def m0(i):
        for k in range(4):
            rs(i, k).start()

    def m1(i):
        p = lax.rem(i, 2)
        for j, owner, rows in ((0, right, lo), (1, left, hi)):
            rs(i, j).wait_recv()
            part[p, owner, rows, :] = (part[p, owner, rows, :].astype(f32) + relay[i, j].astype(f32)).astype(bf16)
        rs(i, 4).start()
        rs(i, 5).start()

    mlp_gain = mlp_gain_ref[...].astype(f32)

    def m2(i):
        p = lax.rem(i, 2)
        for k in range(2, 6):
            rs(i, k).wait_recv()
        for k in range(6):
            rs(i, k).wait_send()
        total = part[p, me].astype(f32) + fin[i, 0].astype(f32) + fin[i, 1].astype(f32)
        hid = (hrow[i].astype(f32) + total).astype(bf16)
        hrow[i] = hid
        nrow[i] = normalize(hid.astype(f32), mlp_gain)
        for c in o_store(i):
            c.start()

    def slot_wait(slot):
        rel, is_sib = slot // 2, slot % 2
        if is_sib:
            for b in range(2):
                sb(rel, b).wait_recv()
        elif rel == 1:
            kx(1).wait_recv()
            sb(1, 1).start()
        elif rel == 2:
            kx(3).wait_recv()
            sb(2, 0).start()
        elif rel == 3:
            kx(4).wait_recv()
            kx(5).wait_recv()
            sb(3, 0).start()
            sb(3, 1).start()

    def chunk(i, carry):
        for kv in range(kv_n):
            m_st[kv] = jnp.full((1, QL), MASK_VALUE, f32)
            l_st[kv] = jnp.zeros((1, QL), f32)
            acc[kv] = jnp.zeros((HEAD_DIM, QL), f32)
        for kv in range(kv_n):
            rows = pl.ds(pl.multiple_of(i * QC, QC), QC)
            attend(i, kv, kbuf[0, 0, kv, rows, :], vbuf[0, 0, kv, :, rows], True)

        def diag_step(j, c2):
            rows = pl.ds(pl.multiple_of(j * QC, QC), QC)
            for kv in range(kv_n):
                attend(i, kv, kbuf[0, 0, kv, rows, :], vbuf[0, 0, kv, :, rows], False)
            return c2
        lax.fori_loop(0, i, diag_step, 0)

        def slot_step(slot, c2):
            rel, is_sib = slot // 2, lax.rem(slot, 2)
            for known in range(1, n_cp):
                @pl.when((i == 0) & (slot == known))
                def _():
                    slot_wait(known)
            from_chip = lax.rem(chip + jnp.where(rel == 1, 3, jnp.where(rel == 2, 1, jnp.where(rel == 3, 2, 0))), n_cp // 2)
            from_core = jnp.where(is_sib == 1, 1 - core, core)

            @pl.when(from_chip * 2 + from_core < cp)
            def _():
                def tile_step(j, c3):
                    rows = pl.ds(pl.multiple_of(j * KEY_TILE, KEY_TILE), KEY_TILE)
                    for kv in range(kv_n):
                        attend(i, kv, kbuf[rel, is_sib, kv, rows, :], vbuf[rel, is_sib, kv, :, rows], False)
                    return c3
                lax.fori_loop(0, tok // KEY_TILE, tile_step, 0)

            @pl.when((i > 0) & (slot == 3))
            def _():
                m1(i - 1)
            return c2
        lax.fori_loop(1, n_cp, slot_step, 0)
        for kv in range(kv_n):
            inv = 1.0 / l_st[kv]
            for g in range(groups):
                lanes = slice(g * QC, (g + 1) * QC)
                h = kv * groups + g
                orow[:, h * HEAD_DIM:(h + 1) * HEAD_DIM] = (acc[kv, :, lanes] * inv[:, lanes]).astype(bf16).T

        @pl.when(i == 0)
        def _():
            wo_load.wait()
        p = lax.rem(i, 2)

        def out_step(j, c2):
            cols = pl.ds(pl.multiple_of(j * OUT_COLS, OUT_COLS), OUT_COLS)
            part[p, :, :, cols] = jnp.dot(orow[...], nbuf[:, cols], preferred_element_type=f32).astype(bf16).reshape(n_tp, R, OUT_COLS)
            return c2
        lax.fori_loop(0, D // OUT_COLS, out_step, 0)
        m0(i)

        @pl.when(i > 0)
        def _():
            h_load(i - 1).wait()
            m2(i - 1)
        return carry
    lax.fori_loop(0, Q_CHUNKS, chunk, 0)
    last = Q_CHUNKS - 1
    m1(last)
    h_load(last).wait()
    m2(last)
    for k in range(6):
        kx(k).wait_send()
    for rel in range(n_cp // 2):
        for b in range(2):
            sb(rel, b).wait_send()
    pltpu.make_async_copy(knat, k_out, kvo_sem.at[0]).wait()
    pltpu.make_async_copy(vnat, v_out, kvo_sem.at[1]).wait()
    for i in range(Q_CHUNKS):
        for c in o_store(i):
            c.wait()


def fused_attention(x, attn_gain, mlp_gain, cos2, sin2, w_q, w_k, w_v, w_o, n_tp, n_cp):
    tok, D = x.shape
    kv_n = w_k.shape[1] // HEAD_DIM
    groups = w_q.shape[1] // w_k.shape[1]
    QC = tok // Q_CHUNKS
    QL = QC * groups
    R = QC // n_tp
    H = R // 2
    bf, f32 = jnp.bfloat16, jnp.float32
    anys = pl.BlockSpec(memory_space=pl.ANY)
    vm = pl.BlockSpec(memory_space=pltpu.VMEM)
    own = tok // n_tp
    dma = pltpu.SemaphoreType.DMA
    return pl.pallas_call(
        functools.partial(attn_kernel, n_tp, n_cp),
        out_shape=(jax.ShapeDtypeStruct((tok, kv_n * HEAD_DIM), bf), jax.ShapeDtypeStruct((tok, kv_n * HEAD_DIM), bf),
                   jax.ShapeDtypeStruct((own, D), bf), jax.ShapeDtypeStruct((own, D), bf)),
        in_specs=[anys, vm, vm, vm, vm, anys, anys, anys, anys],
        out_specs=(anys,) * 4,
        scratch_shapes=[
            pltpu.VMEM((tok, D), bf),
            pltpu.VMEM((2, D, PROJ_TILE), bf),
            pltpu.VMEM((n_cp // 2, 2, kv_n, tok, HEAD_DIM), bf),
            pltpu.VMEM((n_cp // 2, 2, kv_n, HEAD_DIM, tok), bf),
            pltpu.VMEM((Q_CHUNKS, kv_n, HEAD_DIM, QL), bf),
            pltpu.VMEM((2, n_tp, R, D), bf),
            pltpu.VMEM((Q_CHUNKS, 2, H, D), bf),
            pltpu.VMEM((Q_CHUNKS, 2, R, D), bf),
            pltpu.VMEM((Q_CHUNKS, R, D), bf),
            pltpu.VMEM((Q_CHUNKS, R, D), bf),
            pltpu.VMEM((QC, kv_n * groups * HEAD_DIM), bf),
            pltpu.VMEM((kv_n, HEAD_DIM, QL), f32),
            pltpu.VMEM((kv_n, 1, QL), f32),
            pltpu.VMEM((kv_n, 1, QL), f32),
            pltpu.VMEM((tok, kv_n * HEAD_DIM), bf),
            pltpu.VMEM((tok, kv_n * HEAD_DIM), bf),
            dma((Q_CHUNKS,)), dma((2,)), dma, dma((Q_CHUNKS,)), dma((2, Q_CHUNKS)), dma((2,)),
            dma((6,)), dma((6,)), dma((n_cp // 2, 2)), dma((n_cp // 2, 2)), dma((Q_CHUNKS, 6)), dma((Q_CHUNKS, 6)),
        ],
        compiler_params=pltpu.CompilerParams(collective_id=1, has_side_effects=True, vmem_limit_bytes=VMEM_LIMIT),
        name='fused_attention',
    )(x, attn_gain.reshape(1, D), mlp_gain.reshape(1, D), cos2, sin2, w_q, w_k, w_v, w_o)


def mlp_kernel(n_tp, n_hbm, h_ref, wg_hbm, wu_hbm, wd_hbm, out_hbm,
               nbuf, act, wg_buf, wu_buf, wd_buf, part, relay, fin, xfin,
               wsem, dsem, own_sem, ag_send, ag_recv, rs_send, rs_recv, go_send, go_recv, loc_sem):
    me = lax.axis_index('tp')
    right = lax.rem(me + 1, n_tp)
    left = lax.rem(me + n_tp - 1, n_tp)
    _, _, R, D = nbuf.shape
    H = R // 2
    DG = part.shape[-1]
    n_ff = act.shape[1] // FF_TILE
    n_out = D // OUT_TILE
    per_group = DG // OUT_TILE
    lo, hi = pl.ds(0, H), pl.ds(H, H)

    def remote(src, dst, ssem, rsem, to):
        return pltpu.make_async_remote_copy(src_ref=src, dst_ref=dst, send_sem=ssem, recv_sem=rsem,
                                            device_id={'tp': to}, device_id_type=pl.DeviceIdType.MESH)

    def ag(s, k):
        src_slot, dst_slot, rows, to = ((0, 1, lo, right), (0, 1, hi, right), (0, 2, hi, left), (0, 2, lo, left),
                                        (1, 3, lo, right), (2, 3, hi, left))[k]
        return remote(nbuf.at[s, src_slot, rows], nbuf.at[s, dst_slot, rows], ag_send.at[s, k], ag_recv.at[s, k], to)

    def rs(s, g, k):
        src, dst, to = ((part.at[s, g, 3, lo], relay.at[s, g, 0], right),
                        (part.at[s, g, 3, hi], relay.at[s, g, 1], left),
                        (part.at[s, g, 2, hi], fin.at[s, g, 0, hi], right),
                        (part.at[s, g, 1, lo], fin.at[s, g, 1, lo], left),
                        (part.at[s, g, 2, lo], fin.at[s, g, 0, lo], right),
                        (part.at[s, g, 1, hi], fin.at[s, g, 1, hi], left))[k]
        return remote(src, dst, rs_send.at[s, g, k], rs_recv.at[s, g, k], to)

    def out_rows(owner, s, half):
        return pl.ds(pl.multiple_of(((HALVES * s + half) * n_tp + owner) * H, H), H)

    def go(s, g, k):
        cols = pl.ds(g * DG, DG)
        half = (0, 1, 1, 0, 0, 1)[k]
        to = (right, right, left, left, right, left)[k]
        owner = (me, me, me, me, left, right)[k]
        dst = out_hbm.at[out_rows(owner, s, half), cols]
        src = xfin.at[s, g, pl.ds(half * H, H)] if k < 4 else dst
        return remote(src, dst, go_send.at[s, g, k], go_recv.at[s, g, k], to)

    def loc(s, g, half):
        return pltpu.make_async_copy(xfin.at[s, g, pl.ds(half * H, H)], out_hbm.at[out_rows(me, s, half), pl.ds(g * DG, DG)],
                                     loc_sem.at[s, g, half])

    def own(s):
        return pltpu.make_async_copy(n_hbm.at[pl.ds(s * R, R)], nbuf.at[s, 0], own_sem.at[s])

    def gu_load(t, slot):
        cols = pl.ds(pl.multiple_of(t * FF_TILE, FF_TILE), FF_TILE)
        return (pltpu.make_async_copy(wg_hbm.at[:, cols], wg_buf.at[slot], wsem.at[0, slot]),
                pltpu.make_async_copy(wu_hbm.at[:, cols], wu_buf.at[slot], wsem.at[1, slot]))

    def dn_load(j, slot):
        cols = pl.ds(pl.multiple_of(j * OUT_TILE, OUT_TILE), OUT_TILE)
        return pltpu.make_async_copy(wd_hbm.at[:, cols], wd_buf.at[slot], dsem.at[slot])

    def gu_first():
        for t in range(2):
            for c in gu_load(t, t):
                c.start()

    def dn_first():
        for j in range(2):
            dn_load(j, j).start()

    for s in range(HALVES):
        own(s).start()
    gu_first()
    dn_first()
    barrier = pltpu.get_barrier_semaphore()
    for nbr in (left, right):
        pl.semaphore_signal(barrier, inc=1, device_id={'tp': nbr}, device_id_type=pl.DeviceIdType.MESH)
    pl.semaphore_wait(barrier, 2)

    def ag_own(s):
        own(s).wait()
        for k in range(4):
            ag(s, k).start()

    def ag_fwd(s, k):
        ag(s, k).wait_recv()
        ag(s, 4 + k // 2).start()

    def ag_rest(s):
        for k in (1, 3, 4, 5):
            ag(s, k).wait_recv()

    def m0(s, g):
        for k in range(4):
            rs(s, g, k).start()

    def m1(s, g):
        for i, slot, rows in ((0, 2, lo), (1, 1, hi)):
            rs(s, g, i).wait_recv()
            total = part[s, g, slot, rows, :].astype(jnp.float32) + relay[s, g, i].astype(jnp.float32)
            part[s, g, slot, rows, :] = total.astype(jnp.bfloat16)
        rs(s, g, 4).start()
        rs(s, g, 5).start()

    def m2(s, g):
        for k in range(2, 6):
            rs(s, g, k).wait_recv()
        total = (part[s, g, 0].astype(jnp.float32) + fin[s, g, 0].astype(jnp.float32)) + fin[s, g, 1].astype(jnp.float32)
        res = h_ref[pl.ds(s * R, R), pl.ds(g * DG, DG)].astype(jnp.float32)
        xfin[s, g] = (res + total).astype(jnp.bfloat16)
        for k in range(4):
            go(s, g, k).start()
        for half in range(2):
            loc(s, g, half).start()

    def m3(s, g):
        go(s, g, 0).wait_recv()
        go(s, g, 4).start()
        go(s, g, 2).wait_recv()
        go(s, g, 5).start()

    def gate_up(s, hooks):
        def step(t, carry):
            slot = lax.rem(t, 2)
            for c in gu_load(t, slot):
                c.wait()
            rows = nbuf[s].reshape(4 * R, D)
            gate = jnp.dot(rows, wg_buf[slot], preferred_element_type=jnp.float32)
            up = jnp.dot(rows, wu_buf[slot], preferred_element_type=jnp.float32)
            act[:, pl.ds(pl.multiple_of(t * FF_TILE, FF_TILE), FF_TILE)] = (jax.nn.silu(gate) * up).astype(jnp.bfloat16)

            @pl.when(t + 2 < n_ff)
            def _():
                for c in gu_load(t + 2, slot):
                    c.start()
            for at, fn in hooks:
                pl.when(t == at)(fn)
            return carry
        lax.fori_loop(0, n_ff, step, 0)

    def down(s, hooks):
        def step(j, carry):
            slot = lax.rem(j, 2)
            dn_load(j, slot).wait()
            res = jnp.dot(act[...], wd_buf[slot], preferred_element_type=jnp.float32).astype(jnp.bfloat16)
            g, c = j // per_group, lax.rem(j, per_group)
            part[s, g, :, :, pl.ds(pl.multiple_of(c * OUT_TILE, OUT_TILE), OUT_TILE)] = res.reshape(4, R, OUT_TILE)

            @pl.when(j + 2 < n_out)
            def _():
                dn_load(j + 2, slot).start()
            for at, fn in hooks:
                pl.when(j == at)(fn)
            return carry
        lax.fori_loop(0, n_out, step, 0)

    P_ = functools.partial
    G = GROUPS_OUT
    ag_own(0)
    ag_fwd(0, 0)
    ag_fwd(0, 2)
    ag_own(1)
    ag_rest(0)
    gate_up(0, [(6, P_(ag_fwd, 1, 0)), (7, P_(ag_fwd, 1, 2))])
    gu_first()
    send_hooks = lambda s: [(per_group * (g + 1), P_(m0, s, g)) for g in range(G - 1)]
    down(0, send_hooks(0) + [(13, P_(m1, 0, 0)), (18, P_(m1, 0, 1))])
    m0(0, G - 1)
    dn_first()
    ag_rest(1)
    gate_up(1, [(1, P_(m1, 0, 2)), (4, P_(m1, 0, 3))] + [(6 + 2 * g, P_(m2, 0, g)) for g in range(G)])
    down(1, send_hooks(1) + [(per_group * g + 2, P_(m3, 0, g)) for g in range(G)] + [(13, P_(m1, 1, 0)), (18, P_(m1, 1, 1))])
    m0(1, G - 1)
    m1(1, 2)
    m1(1, 3)
    m2(1, 0)
    m2(1, 1)
    m3(1, 0)
    m2(1, 2)
    m3(1, 1)
    m2(1, 3)
    m3(1, 2)
    m3(1, 3)
    for s in range(HALVES):
        for k in range(6):
            ag(s, k).wait_send()
        for g in range(G):
            for half in range(2):
                loc(s, g, half).wait()
            for k in range(6):
                rs(s, g, k).wait_send()
                go(s, g, k).wait_send()
            for k in (1, 3, 4, 5):
                go(s, g, k).wait_recv()


def fused_mlp(normed, hidden, w_gate, w_up, w_down, n_tp):
    own_rows, D = normed.shape
    F = w_gate.shape[1]
    R = own_rows // HALVES
    H = R // 2
    DG = D // GROUPS_OUT
    bf = jnp.bfloat16
    S, G = HALVES, GROUPS_OUT
    anys = pl.BlockSpec(memory_space=pl.ANY)
    vm = pl.BlockSpec(memory_space=pltpu.VMEM)
    return pl.pallas_call(
        functools.partial(mlp_kernel, n_tp),
        out_shape=jax.ShapeDtypeStruct((own_rows * n_tp, D), bf),
        in_specs=[anys, vm, anys, anys, anys],
        out_specs=anys,
        scratch_shapes=[
            pltpu.VMEM((S, 4, R, D), bf),
            pltpu.VMEM((4 * R, F), bf),
            pltpu.VMEM((2, D, FF_TILE), bf),
            pltpu.VMEM((2, D, FF_TILE), bf),
            pltpu.VMEM((2, F, OUT_TILE), bf),
            pltpu.VMEM((S, G, 4, R, DG), bf),
            pltpu.VMEM((S, G, 2, H, DG), bf),
            pltpu.VMEM((S, G, 2, R, DG), bf),
            pltpu.VMEM((S, G, R, DG), bf),
            pltpu.SemaphoreType.DMA((2, 2)),
            pltpu.SemaphoreType.DMA((2,)),
            pltpu.SemaphoreType.DMA((S,)),
            pltpu.SemaphoreType.DMA((S, 6)),
            pltpu.SemaphoreType.DMA((S, 6)),
            pltpu.SemaphoreType.DMA((S, G, 6)),
            pltpu.SemaphoreType.DMA((S, G, 6)),
            pltpu.SemaphoreType.DMA((S, G, 6)),
            pltpu.SemaphoreType.DMA((S, G, 6)),
            pltpu.SemaphoreType.DMA((S, G, 2)),
        ],
        compiler_params=pltpu.CompilerParams(collective_id=0, has_side_effects=True, vmem_limit_bytes=VMEM_LIMIT),
        cost_estimate=pl.CostEstimate(flops=2 * own_rows * n_tp * D * F * 3, bytes_accessed=2 * 3 * 2 * D * F, transcendentals=0),
        name='fused_mlp',
    )(normed, hidden, w_gate, w_up, w_down)


def rope_tables(positions):
    inv_freq = jnp.asarray(ROPE_THETA, jnp.float32) ** (-jnp.arange(0, HEAD_DIM, 2, dtype=jnp.float32) / HEAD_DIM)
    angles = positions.astype(jnp.float32)[:, None] * inv_freq[None, :]
    return jnp.cos(angles), jnp.sin(angles)


def solution(mesh):
    n_tp, n_cp = mesh.shape['tp'], mesh.shape['cp']
    row_spec = P(('dp', 'cp'), None)
    cache_spec = P(('dp', 'cp'), 'tp', None)
    col_spec = P(None, 'tp')
    split_rows = P('tp', None)
    vec_spec = P(None)

    def local_layer(x, attn_gain, w_q, w_k, w_v, w_o, mlp_gain, w_gate, w_up, w_down):
        tok_dev = x.shape[0]
        kv_local = w_k.shape[1] // HEAD_DIM
        cos_tab, sin_tab = rope_tables(lax.axis_index('cp') * tok_dev + jnp.arange(tok_dev))
        cos2 = jnp.concatenate([cos_tab, cos_tab], axis=-1)
        sin2 = jnp.concatenate([-sin_tab, sin_tab], axis=-1)
        keys, values, hidden, normed = fused_attention(x, attn_gain, mlp_gain, cos2, sin2, w_q, w_k, w_v, w_o, n_tp, n_cp)
        x_out = fused_mlp(normed, hidden, w_gate, w_up, w_down, n_tp)
        return x_out, keys.reshape(tok_dev, kv_local, HEAD_DIM), values.reshape(tok_dev, kv_local, HEAD_DIM)

    return jax.shard_map(local_layer, mesh=mesh,
                         in_specs=(row_spec, vec_spec, col_spec, col_spec, col_spec, split_rows, vec_spec, col_spec, col_spec, split_rows),
                         out_specs=(row_spec, cache_spec, cache_spec), check_vma=False)
```

time: 1200 us -> 477 us (0.40)
  matrix products: 480 us -> 0 us
  waiting for transfers between devices: 462 us -> 0 us
  Pallas kernels: 0 us -> 457 us
  other arithmetic: 199 us -> 3.22 us
  local copies, waits for them, and re-layouts: 36.2 us -> 15.3 us
  between operations: 14.8 us -> 0.67 us
    dot_general x39 -> x0, matrix products: 480 us -> none  [the longest x16 176 us: tile_step(): jnp.einsum('kgqs,skd->kgqd', exp_scores.astype(jnp.bfloat16), v_tile, pre...]
    pallas_call x0 -> x2, Pallas kernels: none -> 457 us  [the longest x1 255 us: fused_mlp(): pl.pallas_call(functools.partial(mlp_kernel, n_tp), out_shape=jax.ShapeDt...]
    psum x2 -> x0, waiting for transfers between devices: 377 us -> none  [the longest x1 190 us: local_layer(): attn_total = lax.psum(attn_part, 'tp')]
    reduce_sum x18 -> x0, other arithmetic: 164 us -> none  [the longest x16 148 us: tile_step(): new_sum = run_sum * rescale + jnp.sum(exp_scores, axis=-1)]
    ppermute x14 -> x0, waiting for transfers between devices: 85.5 us -> none  [shift_step(): held = lax.ppermute(held, 'cp', shift_pairs)]
    while x31 -> x0, local copies, waits for them, and re-layouts: 18.9 us -> none
    convert_element_type x4 -> x0, other arithmetic: 16.9 us -> none  [the longest x1 14.1 us: local_layer(): (hidden.astype(jnp.float32) + down_total.astype(jnp.float32)).astype(jnp....]
  transfers between devices with their start and end apart: 16 -> 0, of which waited for: 16 -> 0; matrix products, arithmetic and copies ran while one was open for 0% -> 0% of each run, Pallas kernels for 0% -> 0%
where the time goes in v1:
time: 477 us; the launch traced here: 476 us
  Pallas kernels  457 us (96%)
  local copies, waits for them, and re-layouts  15.3 us (3%)
    pallas_call x1, Pallas kernels, fused_mlp(): pl.pallas_call(functools.partial(mlp_kernel, n_tp), out_shape=jax.ShapeDt...  255 us
    pallas_call x1, Pallas kernels, fused_attention(): pl.pallas_call(functools.partial(attn_kernel, n_tp, n_cp), out_shape=(jax...  201 us

profile of v1, /device:TPU:103, one launch (start us, length us, event | category | flops | bytes accessed | tf_op | source)
XLA Modules:
  0.0 475.9 jit_solution(11854823745142013618)
XLA Ops:
  0.7 1.3 reshape.30.gain_ref
  2.0 1.3 reshape.31.mlp_gain_ref
  3.3 1.9 fusion
  5.2 1.3 pad_maximum_fusion
  6.5 201.3 %fused_attention.1 = (bf16[1024,256]{1,0:T(8,128)(2,1)}, bf16[1024,256]{1,0:T(8,128)(2,1)}, bf16[256,5120]{1,0:T(8,128)(2,1)}, bf16[256,5120]{1,0:T(8,128)(2,1)}) custom-call(bf16[1024,5120]{1,0:T(8,128)(2,1)} %x_hbm.1, bf16[1,5120]{1,0:T(2,128)(2,1)} %reshape.30.gain_ref, bf16[1,5120]{1,0:T(2,128)(2,1)} %reshape.31.mlp_gain_ref, ...), custom_call_target="tpu_custom_call" | custom-call | tf_op jit(solution)/shard_map/fused_attention/pallas_call | solution.py:326
  207.8 2.0 reshape.32
  209.8 2.0 reshape.33
  211.7 255.3 %fused_mlp.1 = bf16[1024,5120]{1,0:T(8,128)(2,1)} custom-call(bf16[256,5120]{1,0:T(8,128)(2,1)} %get-tuple-element.7.n_hbm, bf16[256,5120]{1,0:T(8,128)(2,1)} %get-tuple-element.8.h_ref, bf16[5120,3584]{1,0:T(8,128)(2,1)} %wg_hbm.1, bf16[5120,3584]{1,0:T(8,128)(2,1)} %wu_hbm.1, bf16[3584,5120]{1,0:T(8,128)(2,1)} %wd_hbm.1), custom_call_target="tpu_custom_call" | custom-call | flops 112742891520 | bytes 220200960 | tf_op jit(solution)/shard_map/fused_mlp/pallas_call | solution.py:562
  467.1 8.8 %copy.14 = bf16[1024,5120]{1,0:T(8,128)(2,1)} copy(bf16[1024,5120]{1,0:T(8,128)(2,1)} %fused_mlp.1) | data formatting | bytes 20971520
  (2 shorter events, 0.0 us)

commit v2 on v1

v2 whole, which is shorter than its diff:
```python
import functools
import math
import jax
import jax.numpy as jnp
from jax import lax
from jax.experimental import pallas as pl
from jax.experimental.pallas import tpu as pltpu
from jax.sharding import PartitionSpec as P

HEAD_DIM = 128
OWN, LEFT, RIGHT, FAR = SLOTS = range(4)
LO, HI = BOTH = range(2)
KEY, VALUE = BOTH
KV_A, KV_B = BOTH
ROPE_THETA = 1000000.0
NORM_EPS = 1e-5
MASK_VALUE = -1e30
VMEM_LIMIT = 66000000
HALVES = 2
GROUPS_OUT = 4
COPY_BLOCKS = 16
FF_TILE = 256
OUT_TILE = 256
DN_BUFS = 3
PROJ_TILE = 256
Q_CHUNKS = 4
OUT_COLS = 2560
NORM_ROWS = 16
ANGLE_ROWS = 32


def attn_kernel(n_tp, n_cp, x_hbm, gain_ref, mlp_gain_ref, freq_ref, wq_hbm, wk_hbm, wv_hbm, wo_hbm,
                k_out, v_out, h_out, n_out,
                nbuf, wt, kbuf, vbuf, qt, part, relay, fin, hrow, nrow, orow, s0, s1, acc, m_st, l_st, cos_s, sin_s, bias, vnat, cache,
                xsem, wsem, wosem, hsem, osem, kvo_sem, kx_send, kx_recv, sb_send, sb_recv, rs_send, rs_recv):
    tok, D = nbuf.shape
    kv_n, HT = kbuf.shape[3], kbuf.shape[4]
    QC = tok // Q_CHUNKS
    QL = qt.shape[3]
    groups = QL // QC
    R = QC // n_tp
    H = R // 2
    lo, hi = pl.ds(0, H), pl.ds(H, H)
    me = lax.axis_index('tp')
    right = lax.rem(me + 1, n_tp)
    left = lax.rem(me + n_tp - 1, n_tp)
    far = lax.rem(me + 2, n_tp)
    cp = lax.axis_index('cp')
    core = lax.rem(cp, 2)
    chip = cp // 2
    last_chip = n_cp // 2 - 1
    sib = cp + 1 - 2 * core
    x_right = lax.rem(cp + 2, n_cp)
    x_left = lax.rem(cp + n_cp - 2, n_cp)
    cexp = (HEAD_DIM ** -0.5) * math.log2(math.e)
    f32, bf16 = jnp.float32, jnp.bfloat16
    s_buf = (s0, s1)

    def remote(src, dst, ssem, rsem, to):
        return pltpu.make_async_remote_copy(src_ref=src, dst_ref=dst, send_sem=ssem, recv_sem=rsem,
                                            device_id=to, device_id_type=pl.DeviceIdType.MESH)

    def kx(k, b):
        buf = (kbuf, vbuf)[b]
        src, dst, half, to = ((OWN, LEFT, LO, x_right), (OWN, LEFT, HI, x_right), (OWN, RIGHT, LO, x_left), (OWN, RIGHT, HI, x_left),
                              (LEFT, FAR, LO, x_right), (RIGHT, FAR, HI, x_left))[k]
        return remote(buf.at[src, LO, half], buf.at[dst, LO, half], kx_send.at[k, b], kx_recv.at[k, b], {'cp': to})

    def sb(rel, half, b):
        buf = (kbuf, vbuf)[b]
        return remote(buf.at[rel, LO, half], buf.at[rel, HI, half], sb_send.at[rel, half, b], sb_recv.at[rel, half, b], {'cp': sib})

    def rs(i, k):
        p = lax.rem(i, 2)
        src, dst, to = ((part.at[p, far, lo], relay.at[i, LO], right),
                        (part.at[p, far, hi], relay.at[i, HI], left),
                        (part.at[p, right, hi], fin.at[i, LO, hi], right),
                        (part.at[p, left, lo], fin.at[i, HI, lo], left),
                        (part.at[p, right, lo], fin.at[i, LO, lo], right),
                        (part.at[p, left, hi], fin.at[i, HI, hi], left))[k]
        return remote(src, dst, rs_send.at[i, k], rs_recv.at[i, k], {'tp': to})

    def x_load(c):
        rows = pl.ds(pl.multiple_of(c * QC, QC), QC)
        return pltpu.make_async_copy(x_hbm.at[rows], nbuf.at[rows], xsem.at[c])

    def w_load(ref, t, slot):
        return pltpu.make_async_copy(ref.at[:, pl.ds(pl.multiple_of(t * PROJ_TILE, PROJ_TILE), PROJ_TILE)], wt.at[slot], wsem.at[slot])

    def h_load(i):
        return pltpu.make_async_copy(x_hbm.at[pl.ds(pl.multiple_of(i * QC + me * R, R), R)], hrow.at[i], hsem.at[i])

    def o_store(i):
        rows = pl.ds(i * R, R)
        return (pltpu.make_async_copy(hrow.at[i], h_out.at[rows], osem.at[0, i]),
                pltpu.make_async_copy(nrow.at[i], n_out.at[rows], osem.at[1, i]))

    wo_load = pltpu.make_async_copy(wo_hbm, nbuf, wosem)

    x_load(0).start()
    barrier = pltpu.get_barrier_semaphore()
    for to in ({'tp': left}, {'tp': right}, {'cp': x_left}, {'cp': x_right}, {'cp': sib}):
        pl.semaphore_signal(barrier, inc=1, device_id=to, device_id_type=pl.DeviceIdType.MESH)

    def make_tables():
        freq = freq_ref[...]

        def angles(step, base):
            t = lax.broadcasted_iota(jnp.int32, (ANGLE_ROWS, HEAD_DIM), 0) * step + base
            a = t.astype(f32) * freq
            return jnp.cos(a), jnp.sin(a)

        sign = jnp.where(lax.broadcasted_iota(jnp.int32, (1, HEAD_DIM), 1) < HEAD_DIM // 2, -1.0, 1.0)
        fine_cos, fine_sin = angles(1, 0)
        base_cos, base_sin = angles(ANGLE_ROWS, cp * tok)
        for b in range(tok // ANGLE_ROWS):
            ca, sa = base_cos[b:b + 1], base_sin[b:b + 1]
            rows = slice(b * ANGLE_ROWS, (b + 1) * ANGLE_ROWS)
            cos_s[rows, :] = ca * fine_cos - sa * fine_sin
            sin_s[rows, :] = (sa * fine_cos + ca * fine_sin) * sign

    def make_bias():
        key_at = lax.broadcasted_iota(jnp.int32, bias.shape[1:], 0)
        row_at = lax.broadcasted_iota(jnp.int32, bias.shape[1:], 1)
        for odd in BOTH:
            bias[odd] = jnp.where(key_at <= row_at + odd * QC, 0.0, MASK_VALUE)

    def normalize(wide, gain):
        inv = lax.rsqrt(jnp.mean(wide * wide, axis=-1, keepdims=True) + NORM_EPS)
        return (wide * inv * gain).astype(bf16)

    gain = gain_ref[...].astype(f32)[None, :]

    def stage(c):
        return nrow if c % 2 == 0 else part.at[0]

    def inv_rows(c, b):
        first = (c % 2) * QC + b * NORM_ROWS
        return slice(first, first + NORM_ROWS)

    def stat_chunk(c):
        for b in range(QC // NORM_ROWS):
            rows = slice(c * QC + b * NORM_ROWS, c * QC + (b + 1) * NORM_ROWS)
            wide = nbuf[rows, :].astype(f32)
            s0[inv_rows(c, b), 0:1] = lax.rsqrt(jnp.mean(wide * wide, axis=-1, keepdims=True) + NORM_EPS)

    def norm_chunk(c):
        for b in range(QC // NORM_ROWS):
            rows = slice(c * QC + b * NORM_ROWS, c * QC + (b + 1) * NORM_ROWS)
            scaled = (nbuf[rows, :].astype(f32) * s0[inv_rows(c, b), 0:1] * gain).astype(bf16)
            nbuf[rows, :] = scaled
            stage(c)[b * NORM_ROWS // R, b * NORM_ROWS % R:b * NORM_ROWS % R + NORM_ROWS, :] = scaled

    def rope(u, rows, scale=None):
        wide = u.astype(bf16).astype(f32)
        turned = wide * cos_s[rows, :] + pltpu.roll(wide, HEAD_DIM // 2, 1) * sin_s[rows, :]
        return (turned if scale is None else turned * scale).astype(bf16)

    x_load(0).wait()
    w_load(wk_hbm, 0, 0).start()
    w_load(wv_hbm, 0, 1).start()
    x_load(1).start()
    stat_chunk(0)
    norm_chunk(0)
    x_load(1).wait()
    x_load(2).start()
    x_load(3).start()
    stat_chunk(1)
    w_load(wk_hbm, 0, 0).wait()
    w_load(wv_hbm, 0, 1).wait()
    w_load(wq_hbm, 0, 2).start()
    for i in range(Q_CHUNKS):
        h_load(i).start()
    for c in range(Q_CHUNKS):
        rows = slice(c * QC, (c + 1) * QC)
        half = c // 2
        part_rows = slice((c % 2) * QC, (c % 2 + 1) * QC)
        if c + 2 < Q_CHUNKS:
            x_load(c + 2).wait()
        n_rows = stage(c)[...].reshape(QC, D)
        k_res = jnp.dot(n_rows, wt[0], preferred_element_type=f32)
        v_res = jnp.dot(n_rows, wt[1], preferred_element_type=f32).astype(bf16)
        if c == 0:
            make_tables()
        if c == Q_CHUNKS - 1:
            make_bias()
        if c + 1 < Q_CHUNKS:
            norm_chunk(c + 1)
        if c + 2 < Q_CHUNKS:
            stat_chunk(c + 2)
        vnat[rows, :] = v_res
        for j in range(kv_n):
            cols = slice(j * HEAD_DIM, (j + 1) * HEAD_DIM)
            head = rope(k_res[:, cols], rows)
            kbuf[OWN, LO, half, j, part_rows, :] = head
            vbuf[OWN, LO, half, j, :, part_rows] = v_res[:, cols].T
        if c == 1:
            pl.semaphore_wait(barrier, 5)
            for b in BOTH:
                kx(OWN, b).start()
                kx(2, b).start()
                sb(OWN, LO, b).start()
    w_load(wq_hbm, 1, 0).start()
    w_load(wq_hbm, 2, 1).start()
    for b in BOTH:
        kx(1, b).start()
        kx(3, b).start()
        sb(OWN, HI, b).start()

    n_q = wq_hbm.shape[1] // PROJ_TILE
    heads_tile = PROJ_TILE // HEAD_DIM
    tiles_kv = n_q // kv_n

    def q_step(t, carry):
        slot = lax.rem(t + 2, 3)
        w_load(wq_hbm, t, slot).wait()
        res = jnp.dot(nbuf[...], wt[slot], preferred_element_type=f32)
        kv, base = t // tiles_kv, lax.rem(t, tiles_kv) * heads_tile
        for j in range(heads_tile):
            head = rope(res[:, j * HEAD_DIM:(j + 1) * HEAD_DIM], slice(None), cexp)
            lanes = pl.ds(pl.multiple_of((base + j) * QC, QC), QC)
            for i in range(Q_CHUNKS):
                qt[i, kv, :, lanes] = head[i * QC:(i + 1) * QC].T

        @pl.when(t + 3 < n_q)
        def _():
            w_load(wq_hbm, t + 3, slot).start()
        return carry
    lax.fori_loop(0, n_q, q_step, 0)
    wo_load.start()
    for b in BOTH:
        kx(OWN, b).wait_recv()
        kx(4, b).start()
        sb(LEFT, LO, b).start()
        kx(2, b).wait_recv()
        sb(RIGHT, LO, b).start()
    for half in BOTH:
        for b in BOTH:
            sb(OWN, half, b).wait_recv()

    def ev_near():
        for b in BOTH:
            kx(1, b).wait_recv()
            sb(LEFT, HI, b).start()
            kx(3, b).wait_recv()
            kx(5, b).start()
            sb(RIGHT, HI, b).start()

    def ev_far():
        for b in BOTH:
            kx(4, b).wait_recv()
            sb(FAR, LO, b).start()
            kx(5, b).wait_recv()
            sb(FAR, HI, b).start()

    def ev_sib(rel):
        for half in BOTH:
            for b in BOTH:
                sb(rel, half, b).wait_recv()

    n_far = core + jnp.where(chip >= 1, 2, 0) + jnp.where(chip == last_chip, 2, 0)
    events = ((ev_near, core), (functools.partial(ev_sib, LEFT), core + 1),
              (functools.partial(ev_sib, RIGHT), jnp.where(chip == last_chip, core + 3, n_cp)),
              (ev_far, n_far), (functools.partial(ev_sib, FAR), n_far + 1))

    def block_of(n):
        own = n >= cp
        sib_block = (core == 1) & (n == 0)
        p = n - core
        pair = p // 2
        rel = jnp.where(own | sib_block, OWN, jnp.where(pair == OWN, LEFT, jnp.where(chip == last_chip, pair + 1, FAR)))
        which = jnp.where(own, LO, jnp.where(sib_block, HI, lax.rem(p + 2, 2)))
        return rel, which

    def scores(i, kv, tile, half):
        rel, which = tile
        s_buf[kv][...] = jnp.dot(kbuf[rel, which, half, kv], qt[i, kv], preferred_element_type=f32)

    def soft(kv, tile, half, off=None):
        first = off is not None
        rel, which = tile
        s = s_buf[kv][...]
        if first:
            s = s + jnp.concatenate([bias[off]] * groups, axis=1)
        m_new = jnp.max(s, axis=0, keepdims=True)
        if not first:
            m_old = m_st[kv]
            m_new = jnp.maximum(m_old, m_new)
            alpha = jnp.exp2(m_old - m_new)
        p = jnp.exp2(s - m_new)
        total = jnp.sum(p, axis=0, keepdims=True)
        add = jnp.dot(vbuf[rel, which, half, kv], p.astype(bf16), preferred_element_type=f32)
        m_st[kv] = m_new
        if first:
            l_st[kv] = total
            acc[kv] = add
        else:
            l_st[kv] = l_st[kv] * alpha + total
            acc[kv] = acc[kv] * alpha + add

    def m0(i):
        for k in range(4):
            rs(i, k).start()

    def m1(i):
        p = lax.rem(i, 2)
        for j, owner, rows in ((LO, right, lo), (HI, left, hi)):
            rs(i, j).wait_recv()
            part[p, owner, rows, :] = (part[p, owner, rows, :].astype(f32) + relay[i, j].astype(f32)).astype(bf16)
        rs(i, 4).start()
        rs(i, 5).start()

    mlp_gain = mlp_gain_ref[...].astype(f32)[None, :]

    def m2(i):
        p = lax.rem(i, 2)
        for k in range(2, 6):
            rs(i, k).wait_recv()
        for k in range(6):
            rs(i, k).wait_send()
        total = part[p, me].astype(f32) + fin[i, LO].astype(f32) + fin[i, HI].astype(f32)
        hid = (hrow[i].astype(f32) + total).astype(bf16)
        hrow[i] = hid
        nrow[i] = normalize(hid.astype(f32), mlp_gain)
        for c in o_store(i):
            c.start()

    def chunk(i, carry):
        first, later, before = i == 0, i > 0, i - 1
        def fire(block):
            for fn, at in events:
                @pl.when(first & (at < cp) & (block == at))
                def _():
                    fn()
        own = (0, 0)
        fire(0)
        first_block = block_of(0)
        off = lax.rem(i, 2)
        late = i // 2

        def diag_step(_, c2):
            scores(i, KV_A, own, late)
            scores(i, KV_B, own, late)
            soft(KV_A, own, late, off)
            scores(i, KV_A, (jnp.where(late == 1, 0, first_block[0]), jnp.where(late == 1, 0, first_block[1])), 0)
            soft(KV_B, own, late, off)
            return c2
        lax.fori_loop(0, 1, diag_step, 0)

        def own_step(_, c2):
            scores(i, KV_B, own, LO)
            soft(KV_A, own, LO)
            scores(i, KV_A, first_block, LO)
            soft(KV_B, own, LO)
            return c2
        lax.fori_loop(0, late, own_step, 0)

        def pair_step(n, c2):
            fire(n + 1)

            @pl.when(later & (n == cp // 2))
            def _():
                m1(before)
            blk = block_of(n)
            scores(i, KV_B, blk, LO)
            soft(KV_A, blk, LO)
            scores(i, KV_A, blk, HI)
            soft(KV_B, blk, LO)
            scores(i, KV_B, blk, HI)
            soft(KV_A, blk, HI)
            scores(i, KV_A, block_of(n + 1), LO)
            soft(KV_B, blk, HI)
            return c2
        lax.fori_loop(0, cp, pair_step, 0)

        @pl.when(first)
        def _():
            for fn, at in events:
                pl.when(at >= cp)(fn)
            wo_load.wait()

        @pl.when(later & (cp == 0))
        def _():
            m1(before)
        for kv in range(kv_n):
            inv = 1.0 / l_st[kv]
            for g in range(groups):
                lanes = slice(g * QC, (g + 1) * QC)
                h = kv * groups + g
                orow[:, h * HEAD_DIM:(h + 1) * HEAD_DIM] = (acc[kv, :, lanes] * inv[:, lanes]).astype(bf16).T
        p = lax.rem(i, 2)

        def out_step(j, c2):
            cols = pl.ds(pl.multiple_of(j * OUT_COLS, OUT_COLS), OUT_COLS)
            part[p, :, :, cols] = jnp.dot(orow[...], nbuf[:, cols], preferred_element_type=f32).astype(bf16).reshape(n_tp, R, OUT_COLS)
            return c2
        lax.fori_loop(0, D // OUT_COLS, out_step, 0)
        m0(i)

        @pl.when(later)
        def _():
            h_load(before).wait()
            m2(before)
        return carry
    lax.fori_loop(0, Q_CHUNKS, chunk, 0)
    last = Q_CHUNKS - 1
    for n, out in enumerate((k_out, v_out)):
        for j in range(kv_n):
            if n:
                cache[:, j, :] = vnat[:, j * HEAD_DIM:(j + 1) * HEAD_DIM]
            else:
                for half in BOTH:
                    cache[half * HT:(half + 1) * HT, j, :] = kbuf[OWN, LO, half, j]
        stored = pltpu.make_async_copy(cache, out, kvo_sem.at[n])
        stored.start()
        stored.wait()
    m1(last)
    h_load(last).wait()
    m2(last)
    for b in BOTH:
        for k in range(6):
            kx(k, b).wait_send()
        for rel in range(n_cp // 2):
            for half in BOTH:
                sb(rel, half, b).wait_send()
    for i in range(Q_CHUNKS):
        for c in o_store(i):
            c.wait()


def fused_attention(x, attn_gain, mlp_gain, w_q, w_k, w_v, w_o, n_tp, n_cp):
    tok, D = x.shape
    kv_n = w_k.shape[1] // HEAD_DIM
    groups = w_q.shape[1] // w_k.shape[1]
    QC = tok // Q_CHUNKS
    QL = QC * groups
    R = QC // n_tp
    H = R // 2
    HT = tok // 2
    bf, f32 = jnp.bfloat16, jnp.float32
    anys = pl.BlockSpec(memory_space=pl.ANY)
    vm = pl.BlockSpec(memory_space=pltpu.VMEM)
    own = tok // n_tp
    dma = pltpu.SemaphoreType.DMA
    inv_freq = jnp.asarray(ROPE_THETA, f32) ** (-jnp.arange(0, HEAD_DIM, 2, dtype=f32) / HEAD_DIM)
    freq = jnp.concatenate([inv_freq, inv_freq]).reshape(1, HEAD_DIM)
    return pl.pallas_call(
        functools.partial(attn_kernel, n_tp, n_cp),
        out_shape=(jax.ShapeDtypeStruct((tok, kv_n, HEAD_DIM), bf), jax.ShapeDtypeStruct((tok, kv_n, HEAD_DIM), bf),
                   jax.ShapeDtypeStruct((own, D), bf), jax.ShapeDtypeStruct((own, D), bf)),
        in_specs=[anys, vm, vm, vm, anys, anys, anys, anys],
        out_specs=(anys,) * 4,
        scratch_shapes=[
            pltpu.VMEM((tok, D), bf),
            pltpu.VMEM((3, D, PROJ_TILE), bf),
            pltpu.VMEM((n_cp // 2, 2, 2, kv_n, HT, HEAD_DIM), bf),
            pltpu.VMEM((n_cp // 2, 2, 2, kv_n, HEAD_DIM, HT), bf),
            pltpu.VMEM((Q_CHUNKS, kv_n, HEAD_DIM, QL), bf),
            pltpu.VMEM((2, n_tp, R, D), bf),
            pltpu.VMEM((Q_CHUNKS, 2, H, D), bf),
            pltpu.VMEM((Q_CHUNKS, 2, R, D), bf),
            pltpu.VMEM((Q_CHUNKS, R, D), bf),
            pltpu.VMEM((Q_CHUNKS, R, D), bf),
            pltpu.VMEM((QC, kv_n * groups * HEAD_DIM), bf),
            pltpu.VMEM((HT, QL), f32),
            pltpu.VMEM((HT, QL), f32),
            pltpu.VMEM((kv_n, HEAD_DIM, QL), f32),
            pltpu.VMEM((kv_n, 1, QL), f32),
            pltpu.VMEM((kv_n, 1, QL), f32),
            pltpu.VMEM((tok, HEAD_DIM), f32),
            pltpu.VMEM((tok, HEAD_DIM), f32),
            pltpu.VMEM((2, HT, QC), f32),
            pltpu.VMEM((tok, kv_n * HEAD_DIM), bf),
            pltpu.VMEM((tok, kv_n, HEAD_DIM), bf),
            dma((Q_CHUNKS,)), dma((3,)), dma, dma((Q_CHUNKS,)), dma((2, Q_CHUNKS)), dma((2,)),
            dma((6, 2)), dma((6, 2)), dma((n_cp // 2, 2, 2)), dma((n_cp // 2, 2, 2)), dma((Q_CHUNKS, 6)), dma((Q_CHUNKS, 6)),
        ],
        compiler_params=pltpu.CompilerParams(collective_id=1, has_side_effects=True, vmem_limit_bytes=VMEM_LIMIT),
        name='fused_attention',
    )(x, attn_gain, mlp_gain, freq, w_q, w_k, w_v, w_o)


def mlp_kernel(n_tp, n_hbm, h_hbm, wg_hbm, wu_hbm, wd_hbm, out_hbm,
               nbuf, act, wg_buf, wu_buf, wd_buf, part, relay, fin, xfin, h_ref,
               h_sem, wsem, dsem, own_sem, ag_send, ag_recv, rs_send, rs_recv, go_send, go_recv, loc_sem):
    me = lax.axis_index('tp')
    right = lax.rem(me + 1, n_tp)
    left = lax.rem(me + n_tp - 1, n_tp)
    _, _, R, D = nbuf.shape
    H = R // 2
    DG = part.shape[-1]
    n_ff = act.shape[1] // FF_TILE
    n_out = D // OUT_TILE
    per_group = DG // OUT_TILE
    lo, hi = pl.ds(0, H), pl.ds(H, H)

    def remote(src, dst, ssem, rsem, to):
        return pltpu.make_async_remote_copy(src_ref=src, dst_ref=dst, send_sem=ssem, recv_sem=rsem,
                                            device_id={'tp': to}, device_id_type=pl.DeviceIdType.MESH)

    def ag(s, k):
        src_slot, dst_slot, rows, to = ((OWN, LEFT, lo, right), (OWN, LEFT, hi, right), (OWN, RIGHT, hi, left), (OWN, RIGHT, lo, left),
                                        (LEFT, FAR, lo, right), (RIGHT, FAR, hi, left))[k]
        return remote(nbuf.at[s, src_slot, rows], nbuf.at[s, dst_slot, rows], ag_send.at[s, k], ag_recv.at[s, k], to)

    def rs(s, g, k):
        src, dst, to = ((part.at[s, g, FAR, lo], relay.at[s, g, LO], right),
                        (part.at[s, g, FAR, hi], relay.at[s, g, HI], left),
                        (part.at[s, g, RIGHT, hi], fin.at[s, g, LO, hi], right),
                        (part.at[s, g, LEFT, lo], fin.at[s, g, HI, lo], left),
                        (part.at[s, g, RIGHT, lo], fin.at[s, g, LO, lo], right),
                        (part.at[s, g, LEFT, hi], fin.at[s, g, HI, hi], left))[k]
        return remote(src, dst, rs_send.at[s, g, k], rs_recv.at[s, g, k], to)

    def out_rows(owner, s, half):
        return pl.ds(pl.multiple_of(((HALVES * s + half) * n_tp + owner) * H, H), H)

    def go(s, g, k):
        cols = pl.ds(g * DG, DG)
        half = (LO, HI, HI, LO, LO, HI)[k]
        to = (right, right, left, left, right, left)[k]
        owner = (me, me, me, me, left, right)[k]
        dst = out_hbm.at[out_rows(owner, s, half), cols]
        src = xfin.at[s, g, pl.ds(half * H, H)] if k < 4 else dst
        return remote(src, dst, go_send.at[s, g, k], go_recv.at[s, g, k], to)

    def loc(s, g, half):
        return pltpu.make_async_copy(xfin.at[s, g, pl.ds(half * H, H)], out_hbm.at[out_rows(me, s, half), pl.ds(g * DG, DG)],
                                     loc_sem.at[s, g, half])

    def own(s):
        return pltpu.make_async_copy(n_hbm.at[pl.ds(s * R, R)], nbuf.at[s, 0], own_sem.at[s])

    def gu_load(t, slot):
        cols = pl.ds(pl.multiple_of(t * FF_TILE, FF_TILE), FF_TILE)
        return (pltpu.make_async_copy(wg_hbm.at[:, cols], wg_buf.at[slot], wsem.at[0, slot]),
                pltpu.make_async_copy(wu_hbm.at[:, cols], wu_buf.at[slot], wsem.at[1, slot]))

    def dn_load(j, slot):
        cols = pl.ds(pl.multiple_of(j * OUT_TILE, OUT_TILE), OUT_TILE)
        return pltpu.make_async_copy(wd_hbm.at[:, cols], wd_buf.at[slot], dsem.at[slot])

    def gu_first():
        for t in range(2):
            for c in gu_load(t, t):
                c.start()

    def dn_first():
        for j in range(DN_BUFS):
            dn_load(j, j).start()

    for s in range(HALVES):
        own(s).start()
    gu_first()
    barrier = pltpu.get_barrier_semaphore()
    for nbr in (left, right):
        pl.semaphore_signal(barrier, inc=1, device_id={'tp': nbr}, device_id_type=pl.DeviceIdType.MESH)
    pl.semaphore_wait(barrier, 2)

    def ag_own(s):
        own(s).wait()
        for k in range(4):
            ag(s, k).start()

    def ag_fwd(s, k):
        ag(s, k).wait_recv()
        ag(s, 4 + k // 2).start()

    def ag_rest(s):
        for k in (1, 3, 4, 5):
            ag(s, k).wait_recv()

    def m0(s, g):
        for k in range(4):
            rs(s, g, k).start()

    def m1(s, g):
        for i, slot, rows in ((LO, RIGHT, lo), (HI, LEFT, hi)):
            rs(s, g, i).wait_recv()
            total = part[s, g, slot, rows, :].astype(jnp.float32) + relay[s, g, i].astype(jnp.float32)
            part[s, g, slot, rows, :] = total.astype(jnp.bfloat16)
        rs(s, g, 4).start()
        rs(s, g, 5).start()

    def m2(s, g):
        for k in range(2, 6):
            rs(s, g, k).wait_recv()
        total = (part[s, g, OWN].astype(jnp.float32) + fin[s, g, LO].astype(jnp.float32)) + fin[s, g, HI].astype(jnp.float32)
        res = h_ref[pl.ds(s * R, R), pl.ds(g * DG, DG)].astype(jnp.float32)
        xfin[s, g] = (res + total).astype(jnp.bfloat16)
        for k in range(4):
            go(s, g, k).start()
        for half in BOTH:
            loc(s, g, half).start()

    def m3(s, g):
        go(s, g, 0).wait_recv()
        go(s, g, 4).start()
        go(s, g, 2).wait_recv()
        go(s, g, 5).start()

    def gate_up(s, first, count, hooks):
        def step(t, carry):
            slot = lax.rem(t, 2)
            for c in gu_load(t, slot):
                c.wait()
            rows = nbuf[s, first:first + count].reshape(count * R, D)
            gate = jnp.dot(rows, wg_buf[slot], preferred_element_type=jnp.float32)
            up = jnp.dot(rows, wu_buf[slot], preferred_element_type=jnp.float32)
            act[first * R:(first + count) * R, pl.ds(pl.multiple_of(t * FF_TILE, FF_TILE), FF_TILE)] = (jax.nn.silu(gate) * up).astype(jnp.bfloat16)

            @pl.when(t + 2 < n_ff)
            def _():
                for c in gu_load(t + 2, slot):
                    c.start()
            for at, fn in hooks:
                pl.when(t == at)(fn)
            return carry
        lax.fori_loop(0, n_ff, step, 0)

    def down(s, hooks):
        def step(j, carry):
            slot = lax.rem(j, DN_BUFS)
            dn_load(j, slot).wait()
            res = jnp.dot(act[...], wd_buf[slot], preferred_element_type=jnp.float32).astype(jnp.bfloat16)
            g, c = j // per_group, lax.rem(j, per_group)
            part[s, g, :, :, pl.ds(pl.multiple_of(c * OUT_TILE, OUT_TILE), OUT_TILE)] = res.reshape(4, R, OUT_TILE)

            @pl.when(j + DN_BUFS < n_out)
            def _():
                dn_load(j + DN_BUFS, slot).start()
            for at, fn in hooks:
                pl.when(j == at)(fn)
            return carry
        lax.fori_loop(0, n_out, step, 0)

    P_ = functools.partial
    G = GROUPS_OUT
    ag_own(0)

    def feed():
        ag_fwd(0, 0)
        ag_fwd(0, 2)
        ag_own(1)
    dn_first()
    h_load = pltpu.make_async_copy(h_hbm, h_ref, h_sem)
    h_load.start()
    gate_up(0, 0, 1, [(7, feed)])
    h_load.wait()
    gu_first()
    ag_rest(0)
    gate_up(0, 1, 3, [(7, P_(ag_fwd, 1, 0)), (8, P_(ag_fwd, 1, 2))])
    gu_first()
    send_hooks = lambda s: [(per_group * (g + 1), P_(m0, s, g)) for g in range(G - 1)]
    down(0, send_hooks(0) + [(13, P_(m1, 0, 0)), (18, P_(m1, 0, 1))])
    m0(0, G - 1)
    dn_first()
    ag_rest(1)
    gate_up(1, 0, 4, [(1, P_(m1, 0, 2)), (4, P_(m1, 0, 3))] + [(6 + 2 * g, P_(m2, 0, g)) for g in range(G)])
    down(1, send_hooks(1) + [(per_group * g + 2, P_(m3, 0, g)) for g in range(G)] + [(13, P_(m1, 1, 0)), (18, P_(m1, 1, 1))])
    m0(1, G - 1)
    m1(1, 2)
    m1(1, 3)
    m2(1, 0)
    m2(1, 1)
    m3(1, 0)
    m2(1, 2)
    m3(1, 1)
    m2(1, 3)
    m3(1, 2)
    m3(1, 3)
    for s in range(HALVES):
        for k in range(6):
            ag(s, k).wait_send()
        for g in range(G):
            for half in BOTH:
                loc(s, g, half).wait()
            for k in range(6):
                rs(s, g, k).wait_send()
                go(s, g, k).wait_send()
            for k in (1, 3, 4, 5):
                go(s, g, k).wait_recv()


def fused_mlp(normed, hidden, w_gate, w_up, w_down, n_tp):
    own_rows, D = normed.shape
    F = w_gate.shape[1]
    R = own_rows // HALVES
    H = R // 2
    DG = D // GROUPS_OUT
    bf = jnp.bfloat16
    S, G = HALVES, GROUPS_OUT
    anys = pl.BlockSpec(memory_space=pl.ANY)
    return pl.pallas_call(
        functools.partial(mlp_kernel, n_tp),
        out_shape=jax.ShapeDtypeStruct((own_rows * n_tp, D), bf),
        in_specs=[anys] * 5,
        out_specs=anys,
        scratch_shapes=[
            pltpu.VMEM((S, 4, R, D), bf),
            pltpu.VMEM((4 * R, F), bf),
            pltpu.VMEM((2, D, FF_TILE), bf),
            pltpu.VMEM((2, D, FF_TILE), bf),
            pltpu.VMEM((DN_BUFS, F, OUT_TILE), bf),
            pltpu.VMEM((S, G, 4, R, DG), bf),
            pltpu.VMEM((S, G, 2, H, DG), bf),
            pltpu.VMEM((S, G, 2, R, DG), bf),
            pltpu.VMEM((S, G, R, DG), bf),
            pltpu.VMEM((own_rows, D), bf),
            pltpu.SemaphoreType.DMA,
            pltpu.SemaphoreType.DMA((2, 2)),
            pltpu.SemaphoreType.DMA((DN_BUFS,)),
            pltpu.SemaphoreType.DMA((S,)),
            pltpu.SemaphoreType.DMA((S, 6)),
            pltpu.SemaphoreType.DMA((S, 6)),
            pltpu.SemaphoreType.DMA((S, G, 6)),
            pltpu.SemaphoreType.DMA((S, G, 6)),
            pltpu.SemaphoreType.DMA((S, G, 6)),
            pltpu.SemaphoreType.DMA((S, G, 6)),
            pltpu.SemaphoreType.DMA((S, G, 2)),
        ],
        compiler_params=pltpu.CompilerParams(collective_id=0, has_side_effects=True, vmem_limit_bytes=VMEM_LIMIT),
        cost_estimate=pl.CostEstimate(flops=2 * own_rows * n_tp * D * F * 3, bytes_accessed=2 * 3 * 2 * D * F, transcendentals=0),
        name='fused_mlp',
    )(normed, hidden, w_gate, w_up, w_down)


def hand_over_kernel(x_in, k_in, v_in, x_out, k_out, v_out, x_buf, k_buf, v_buf, in_sem, out_sem):
    n_blocks, rows, _ = x_buf.shape
    copies = []
    for b in range(n_blocks):
        at = pl.ds(b * rows, rows)
        copies.append((pltpu.make_async_copy(x_in.at[at], x_buf.at[b], in_sem.at[b]), pltpu.make_async_copy(x_buf.at[b], x_out.at[at], out_sem.at[b])))
    for n, (src, buf, dst) in enumerate(((k_in, k_buf, k_out), (v_in, v_buf, v_out))):
        copies.append((pltpu.make_async_copy(src, buf, in_sem.at[n_blocks + n]), pltpu.make_async_copy(buf, dst, out_sem.at[n_blocks + n])))
    for load, _ in copies:
        load.start()
    for load, store in copies:
        load.wait()
        store.start()
    for _, store in copies:
        store.wait()


def hand_over(x_out, keys, values):
    rows, D = x_out.shape
    bf = jnp.bfloat16
    block = rows // COPY_BLOCKS
    anys = pl.BlockSpec(memory_space=pl.ANY)
    dma = pltpu.SemaphoreType.DMA((COPY_BLOCKS + 2,))
    return pl.pallas_call(
        hand_over_kernel,
        out_shape=tuple(jax.ShapeDtypeStruct(a.shape, bf) for a in (x_out, keys, values)),
        in_specs=[anys] * 3,
        out_specs=(anys,) * 3,
        scratch_shapes=[pltpu.VMEM((COPY_BLOCKS, block, D), bf), pltpu.VMEM(keys.shape, bf), pltpu.VMEM(values.shape, bf), dma, dma],
        compiler_params=pltpu.CompilerParams(vmem_limit_bytes=VMEM_LIMIT),
        name='hand_over',
    )(x_out, keys, values)


def solution(mesh):
    n_tp, n_cp = mesh.shape['tp'], mesh.shape['cp']
    row_spec = P(('dp', 'cp'), None)
    cache_spec = P(('dp', 'cp'), 'tp', None)
    col_spec = P(None, 'tp')
    split_rows = P('tp', None)
    vec_spec = P(None)

    def local_layer(x, attn_gain, w_q, w_k, w_v, w_o, mlp_gain, w_gate, w_up, w_down):
        keys, values, hidden, normed = fused_attention(x, attn_gain, mlp_gain, w_q, w_k, w_v, w_o, n_tp, n_cp)
        x_out = fused_mlp(normed, hidden, w_gate, w_up, w_down, n_tp)
        return hand_over(x_out, keys, values)

    return jax.shard_map(local_layer, mesh=mesh,
                         in_specs=(row_spec, vec_spec, col_spec, col_spec, col_spec, split_rows, vec_spec, col_spec, col_spec, split_rows),
                         out_specs=(row_spec, cache_spec, cache_spec), check_vma=False)
```

time: 477 us -> 422 us (0.88)
  Pallas kernels: 457 us -> 420 us
  local copies, waits for them, and re-layouts: 15.3 us -> 0 us
    pallas_call x1, Pallas kernels: 201 us -> 153 us  [fused_attention(): pl.pallas_call(functools.partial(attn_kernel, n_tp, n_cp), out_shape=(jax...]
    unnamed x1 -> x0, local copies, waits for them, and re-layouts: 8.78 us -> none
    pallas_call x0 -> x1, Pallas kernels: none -> 8.57 us  [hand_over(): pl.pallas_call(hand_over_kernel, out_shape=tuple((jax.ShapeDtypeStruct(a....]
    reshape x4 -> x0, local copies, waits for them, and re-layouts: 6.55 us -> none  [the longest x1 1.96 us: local_layer(): keys.reshape(tok_dev, kv_local, HEAD_DIM)]
where the time goes in v2:
time: 422 us
  Pallas kernels  420 us (100%)
    pallas_call x1, Pallas kernels, fused_mlp(): pl.pallas_call(functools.partial(mlp_kernel, n_tp), out_shape=jax.ShapeDt...  259 us
    pallas_call x1, Pallas kernels, fused_attention(): pl.pallas_call(functools.partial(attn_kernel, n_tp, n_cp), out_shape=(jax...  153 us
    pallas_call x1, Pallas kernels, hand_over(): pl.pallas_call(hand_over_kernel, out_shape=tuple((jax.ShapeDtypeStruct(a....  8.57 us

profile of v2, /device:TPU:103, one launch (start us, length us, event | category | flops | bytes accessed | tf_op | source)
XLA Modules:
  0.0 421.8 jit_solution(9310162512344372685)
XLA Ops:
  0.6 0.6 maximum_bitcast_fusion.freq_ref
  1.2 153.1 %fused_attention.1 = (bf16[1024,2,128]{2,1,0:T(2,128)(2,1)}, bf16[1024,2,128]{2,1,0:T(2,128)(2,1)}, bf16[256,5120]{1,0:T(8,128)(2,1)}, bf16[256,5120]{1,0:T(8,128)(2,1)}) custom-call(bf16[1024,5120]{1,0:T(8,128)(2,1)} %x_hbm.1, bf16[5120]{0:T(1024)(128)(2,1)} %gain_ref.1, bf16[5120]{0:T(1024)(128)(2,1)} %mlp_gain_ref.1, ...), custom_call_target="tpu_custom_call" | custom-call | tf_op jit(solution)/shard_map/fused_attention/pallas_call | solution.py:447
  154.3 258.7 %fused_mlp.1.x_in = bf16[1024,5120]{1,0:T(8,128)(2,1)} custom-call(bf16[256,5120]{1,0:T(8,128)(2,1)} %get-tuple-element.7.n_hbm, bf16[256,5120]{1,0:T(8,128)(2,1)} %get-tuple-element.8.h_hbm, bf16[5120,3584]{1,0:T(8,128)(2,1)} %wg_hbm.1, bf16[5120,3584]{1,0:T(8,128)(2,1)} %wu_hbm.1, bf16[3584,5120]{1,0:T(8,128)(2,1)} %wd_hbm.1), custom_call_target="tpu_custom_call" | custom-call | flops 112742891520 | bytes 220200960 | tf_op jit(solution)/shard_map/fused_mlp/pallas_call | solution.py:694
  413.1 8.6 %hand_over.1 = (bf16[1024,5120]{1,0:T(8,128)(2,1)}, bf16[1024,2,128]{2,1,0:T(2,128)(2,1)}, bf16[1024,2,128]{2,1,0:T(2,128)(2,1)}) custom-call(bf16[1024,5120]{1,0:T(8,128)(2,1)} %fused_mlp.1.x_in, bf16[1024,2,128]{2,1,0:T(2,128)(2,1)} %get-tuple-element.9.k_in, bf16[1024,2,128]{2,1,0:T(2,128)(2,1)} %get-tuple-element.10.v_in), custom_call_target="tpu_custom_call" | custom-call | tf_op jit(solution)/shard_map/hand_over/pallas_call | solution.py:751
  (1 shorter events, 0.0 us)
